TPU v7x, 256 devices: a whole 4x4x8 slice. The times are simulated.
256 devices in a mesh: lat: 64 (over z_hi, y, x, core), ens: 4 (over z_lo).
Axes of the slice: x: 4, y: 4, z: 8 (z_hi: 2, z_lo: 4; z = z_hi * 4 + z_lo), core: 2. Of those that a mesh axis runs over, the one named last changes fastest.
Arguments:
- predicted_grid: bfloat16 [8, 36, 512, 1440], P('ens', None, 'lat'), may hold values from -6 to 6
- verifying_coefficients: float32 [36, 2, 128, 721], P(None, None, 'lat'), may hold values from -5 to 5
- weighted_polynomial_values: bfloat16 [128, 512, 721], P('lat'), may hold values from -0.25 to 0.25
- zonal_order_values: int32 [128], replicated, may hold values from 0 to 720, as said below
Outputs:
- prediction_sensitivity: bfloat16 [8, 36, 512, 1440], P('ens', None, 'lat')
- coefficient_error_mean: float32 [36, 2, 128], P(None, None, 'lat')
Inputs may be any that keep to these rules, and one draw needn't show every extreme that they name: `zonal_order_values`: the wavenumbers are distinct, 0 and 720 are always among them; slot s belongs to index s // 2 of lat.
All inputs are finite; a program needn't handle non-finite values.
Results may differ from a plain program's by a relative error of at most 0.014.
Values may be sent and summed in bfloat16 or wider, within the bound.
No kernel may reach another device: no remote copies, remote signals or barrier semaphores. Data moves between devices by JAX's collectives and lax.ppermute only.
A program may use at most 64 MiB of HBM per device.

v0:
```python
import math

import jax
import jax.numpy as jnp
from jax import lax
from jax.sharding import PartitionSpec as P

smooth_width = 0.1


def fourier_table(zonal_order_values, meridian_node_number):
    lon_index = jnp.arange(meridian_node_number, dtype=jnp.int32)
    phases = lon_index[:, None] * zonal_order_values[None, :] % meridian_node_number
    angles = 2.0 * math.pi / meridian_node_number * phases.astype(jnp.float32)
    zonal_order_lookup = jnp.stack([jnp.cos(angles), -jnp.sin(angles)], axis=2)
    return zonal_order_lookup.reshape(meridian_node_number, -1).astype(jnp.bfloat16)


def degree_weights(zonal_order_values, degree_count):
    degrees = jnp.arange(degree_count, dtype=jnp.int32)
    factor = jnp.where(zonal_order_values == 0, 1.0, 2.0).astype(jnp.float32)
    active = (degrees[None, :] >= zonal_order_values[:, None]).astype(jnp.float32)
    return factor[:, None] * active


def soft_abs(values):
    return jnp.sqrt(values * values + smooth_width * smooth_width) - smooth_width


def soft_sign(values):
    return values / jnp.sqrt(values * values + smooth_width * smooth_width)


def pair_terms(own_coeffs, all_coeffs):
    gaps = own_coeffs[:, :, None, :] - all_coeffs[:, None, :, :]
    return (jnp.sum(soft_abs(gaps), axis=2), jnp.sum(soft_sign(gaps), axis=2))


def body(predicted_grid, verifying_coefficients, weighted_polynomial_values, zonal_order_values):
    realization_total, variable_number, parallel_line_block, meridian_node_number = (
        predicted_grid.shape
    )
    grid_node_number, parallel_line_number, degree_count = weighted_polynomial_values.shape
    wave_count = zonal_order_values.shape[0]
    realization_pile = realization_total * lax.axis_size("ens")
    zonal_order_lookup = fourier_table(zonal_order_values, meridian_node_number)
    divisor_factor = meridian_node_number ** (-0.5)
    sphere_coefficient_sets = (
        jnp.dot(
            predicted_grid.reshape(-1, meridian_node_number),
            zonal_order_lookup,
            preferred_element_type=jnp.float32,
        )
        * divisor_factor
    )
    sphere_coefficient_sets = sphere_coefficient_sets.astype(jnp.bfloat16).reshape(
        realization_total, variable_number, parallel_line_block, 2 * wave_count
    )
    sphere_coefficient_sets = lax.all_to_all(
        sphere_coefficient_sets, "lat", split_axis=3, concat_axis=2, tiled=True
    )
    sphere_coefficient_sets = lax.all_to_all(
        sphere_coefficient_sets, "ens", split_axis=1, concat_axis=0, tiled=True
    )
    held_members = sphere_coefficient_sets.shape[0]
    held_vars = sphere_coefficient_sets.shape[1]
    sphere_coefficient_sets = sphere_coefficient_sets.reshape(
        held_members, held_vars, parallel_line_number, grid_node_number, 2
    )
    coeffs = jnp.einsum(
        "mvlsr,sln->vrsmn",
        sphere_coefficient_sets,
        weighted_polynomial_values,
        preferred_element_type=jnp.float32,
    )
    row_count = held_vars * 2 * grid_node_number
    coeffs = coeffs.reshape(row_count, held_members, degree_count)
    own_waves = lax.dynamic_slice_in_dim(
        zonal_order_values, lax.axis_index("lat") * grid_node_number, grid_node_number
    )
    weights = jnp.broadcast_to(
        degree_weights(own_waves, degree_count)[None, None],
        (held_vars, 2, grid_node_number, degree_count),
    )
    weights = weights.reshape(row_count, degree_count)
    observed = lax.dynamic_slice_in_dim(
        verifying_coefficients, lax.axis_index("ens") * held_vars, held_vars, 0
    ).reshape(row_count, degree_count)
    spread_abs, spread_sign = pair_terms(coeffs, coeffs)
    misses = coeffs - observed[:, None, :]
    scores = jnp.sum(soft_abs(misses), axis=1) / realization_pile - jnp.sum(spread_abs, axis=1) / (
        2 * realization_pile * realization_pile
    )
    local_totals = jnp.sum(weights * scores, axis=1) / degree_count
    probability_error_sums = lax.all_gather(local_totals, "ens", axis=0, tiled=True)
    gradients = (
        weights[:, None, :]
        * (
            soft_sign(misses) / realization_pile
            - spread_sign / (realization_pile * realization_pile)
        )
    ).astype(jnp.bfloat16)
    gradients = gradients.reshape(held_vars, 2, grid_node_number, held_members, degree_count)
    returned = jnp.einsum(
        "vrsmn,sln->mvlsr",
        gradients,
        weighted_polynomial_values,
        preferred_element_type=jnp.float32,
    ).astype(jnp.bfloat16)
    returned = returned.reshape(held_members, held_vars, parallel_line_number, 2 * grid_node_number)
    returned = lax.all_to_all(returned, "ens", split_axis=0, concat_axis=1, tiled=True)
    returned = lax.all_to_all(returned, "lat", split_axis=2, concat_axis=3, tiled=True)
    sensitivity_grid = (
        lax.dot_general(
            returned.reshape(-1, 2 * wave_count),
            zonal_order_lookup,
            (((1,), (1,)), ((), ())),
            preferred_element_type=jnp.float32,
        )
        * divisor_factor
    )
    prediction_sensitivity = sensitivity_grid.astype(jnp.bfloat16).reshape(predicted_grid.shape)
    return (
        prediction_sensitivity,
        probability_error_sums.reshape(variable_number, 2, grid_node_number),
    )


def solution(mesh):
    placed = (P("ens", None, "lat", None), P(None, None, "lat", None), P("lat", None, None), P())
    return jax.shard_map(
        body,
        mesh=mesh,
        in_specs=placed,
        out_specs=(P("ens", None, "lat", None), P(None, None, "lat")),
        check_vma=False,
    )
```

profile of v0, /device:TPU:1, one launch (start us, length us, event | category | flops | bytes accessed | tf_op | source)
XLA Modules:
  0.0 128.5 jit_solution(6234359489161493280)
XLA Ops:
  0.6 0.0 copy-start
  0.6 4.1 %cosine_convert_fusion = (bf16[1440,128,1]{1,0,2:T(8,128)(2,1)S(1)}, bf16[1440,128,1]{1,0,2:T(8,128)(2,1)S(1)}) fusion(s32[128]{0:T(128)} %param.7), kind=kLoop, calls=%fused_computation.27 | loop fusion | flops 2211840 | bytes 737792 | tf_op jit(solution)/shard_map/convert
  4.8 0.1 pad_maximum_fusion
  4.8 1.0 copy.123
  5.8 0.6 convert_element_type.49
  6.4 0.0 copy-done
  6.4 0.0 copy-start.1
  6.4 0.7 fusion.12
  7.1 0.3 copy-done.1
  7.3 1.1 copy.124
  8.4 3.2 %reshape.195 = bf16[64,2,1152]{2,1,0:T(2,128)(2,1)} reshape(bf16[256,2,8,36]{3,2,1,0:T(8,128)(2,1)S(1)} %bitcast.53) | data formatting | bytes 589824
  11.6 15.6 %all-to-all-start = ((bf16[64,2,1152]{2,1,0:T(2,128)(2,1)}), bf16[64,2,1152]{2,1,0:T(2,128)(2,1)S(1)}, u32[]{:S(2)}, u32[]{:S(2)}) async-start(bf16[64,2,1152]{2,1,0:T(2,128)(2,1)} %reshape.195), calls=%async_computation | async-start | bytes 589824 | tf_op jit(solution)/shard_map/all_to_all | solution.py:59
  27.2 13.9 %all-to-all-done = bf16[64,2,1152]{2,1,0:T(2,128)(2,1)S(1)} async-done(((bf16[64,2,1152]{2,1,0:T(2,128)(2,1)}), bf16[64,2,1152]{2,1,0:T(2,128)(2,1)S(1)}, u32[]{:S(2)}, u32[]{:S(2)}) %all-to-all-start) | async-done | bytes 294944 | tf_op jit(solution)/shard_map/all_to_all | solution.py:59
  41.1 3.0 %reshape.196 = bf16[256,2,8,36]{3,2,1,0:T(8,128)(2,1)S(1)} reshape(bf16[64,2,1152]{2,1,0:T(2,128)(2,1)S(1)} %all-to-all-done) | data formatting | bytes 589824
  44.1 0.0 copy-start.3
  44.1 1.2 copy.171
  45.3 2.2 %copy.127 = bf16[2,36,512,4]{2,3,0,1:T(4,128)(2,1)} copy(bf16[2,36,512,4]{1,2,3,0:T(8,128)(2,1)} %bitcast.55) | data formatting | bytes 589824 | tf_op jit(solution)/shard_map/all_to_all | solution.py:59
  47.5 5.6 %all-to-all-start.1 = ((bf16[2,36,512,4]{2,3,0,1:T(4,128)(2,1)}), bf16[2,36,512,4]{2,3,0,1:T(4,128)(2,1)S(1)}, u32[]{:S(2)}, u32[]{:S(2)}) async-start(bf16[2,36,512,4]{2,3,0,1:T(4,128)(2,1)} %copy.127), calls=%async_computation.1 | async-start | bytes 589824 | tf_op jit(solution)/shard_map/all_to_all | solution.py:62
  53.1 0.0 copy-done.3
  53.1 0.1 compare_select_fusion.1
  53.2 0.9 constant_dynamic-slice_fusion
  54.1 0.1 compare_select_fusion
  54.2 7.0 %all-to-all-done.1 = bf16[2,36,512,4]{2,3,0,1:T(4,128)(2,1)S(1)} async-done(((bf16[2,36,512,4]{2,3,0,1:T(4,128)(2,1)}), bf16[2,36,512,4]{2,3,0,1:T(4,128)(2,1)S(1)}, u32[]{:S(2)}, u32[]{:S(2)}) %all-to-all-start.1) | async-done | bytes 294944 | tf_op jit(solution)/shard_map/all_to_all | solution.py:62
  61.2 0.2 copy.129
  61.5 0.1 reshape.183
  61.6 2.0 %fusion.7 = f32[2,8,9,2,721]{4,1,0,3,2:T(8,128)S(1)} fusion(bf16[2,512,721,1,1]{1,0,2,4,3:T(2,128)(2,1)} %bitcast.67, bf16[8,9,512,2,2]{2,0,4,3,1:T(8,128)(2,1)S(1)} %reshape.183), kind=kOutput, calls=%fused_computation.10 | convolution fusion | flops 212631552 | bytes 2602112 | tf_op jit(solution)/shard_map/mvlsr,sln->vrsmn/dot_general | solution.py:70
  63.6 6.5 %fusion.4 = (f32[36,721]{1,0:T(8,128)S(1)}, f32[36,8,721]{2,1,0:T(8,128)S(1)}) fusion(f32[36,8,721]{2,1,0:T(8,128)S(1)} %bitcast.65), kind=kLoop, calls=%fused_computation.6 | loop fusion | flops 11394684 | bytes 1765008 | tf_op jit(solution)/shard_map/reduce_sum | solution.py:91
  70.1 0.0 copy-start.4
  70.1 0.1 broadcast_multiply_fusion
  70.2 0.8 add_reduce_fusion
  71.0 0.5 copy-done.4
  71.5 0.0 copy-start.5
  71.5 0.4 fusion.13
  72.0 0.9 copy.136
  72.8 4.5 %all-to-all-start.2 = ((bf16[8,9,512,4]{2,3,1,0:T(4,128)(2,1)}), bf16[8,9,512,4]{2,3,1,0:T(4,128)(2,1)S(1)}, u32[]{:S(2)}, u32[]{:S(2)}) async-start(bf16[8,9,512,4]{2,3,1,0:T(4,128)(2,1)} %copy.136), calls=%async_computation.2 | async-start | bytes 589824 | tf_op jit(solution)/shard_map/all_to_all | solution.py:111
  77.4 0.1 broadcast_in_dim.24
  77.5 0.0 copy-done.5
  77.5 0.6 dynamic-slice
  78.7 6.7 %all-to-all-done.2 = bf16[8,9,512,4]{2,3,1,0:T(4,128)(2,1)S(1)} async-done(((bf16[8,9,512,4]{2,3,1,0:T(4,128)(2,1)}), bf16[8,9,512,4]{2,3,1,0:T(4,128)(2,1)S(1)}, u32[]{:S(2)}, u32[]{:S(2)}) %all-to-all-start.2) | async-done | bytes 294944 | tf_op jit(solution)/shard_map/all_to_all | solution.py:111
  85.4 0.1 copy.137
  85.5 0.8 copy.138
  86.3 3.2 %reshape.197 = bf16[64,2,1152]{2,1,0:T(2,128)(2,1)} reshape(bf16[512,2,4,36]{3,2,1,0:T(4,128)(2,1)S(1)} %bitcast.56) | data formatting | bytes 589824
  89.6 6.6 %all-to-all-start.3 = ((bf16[64,2,1152]{2,1,0:T(2,128)(2,1)}), bf16[64,2,1152]{2,1,0:T(2,128)(2,1)S(1)}, u32[]{:S(2)}, u32[]{:S(2)}) async-start(bf16[64,2,1152]{2,1,0:T(2,128)(2,1)} %reshape.197), calls=%async_computation.3 | async-start | bytes 589824 | tf_op jit(solution)/shard_map/all_to_all | solution.py:112
  96.2 0.1 copy.142
  96.3 0.1 div.50
  96.3 0.1 multiply_reduce_fusion
  96.5 0.1 multiply_dynamic-update-slice_fusion
  96.6 11.2 %all-reduce = f32[144]{0:T(256)S(1)} all-reduce(f32[144]{0:T(256)S(1)} %multiply_dynamic-update-slice_fusion), channel_id=1, replica_groups=mesh['lat'=64,'ens'=4] {'ens'}, use_global_device_ids=true, to_apply=%add | all-reduce | flops 144 | bytes 1152
  107.8 0.2 reshape.187
  108.0 0.7 copy.143
  108.7 1.9 %all-to-all-done.3 = bf16[64,2,1152]{2,1,0:T(2,128)(2,1)S(1)} async-done(((bf16[64,2,1152]{2,1,0:T(2,128)(2,1)}), bf16[64,2,1152]{2,1,0:T(2,128)(2,1)S(1)}, u32[]{:S(2)}, u32[]{:S(2)}) %all-to-all-start.3) | async-done | bytes 294944 | tf_op jit(solution)/shard_map/all_to_all | solution.py:112
  110.6 3.0 %reshape.198 = bf16[512,2,4,36]{3,2,1,0:T(4,128)(2,1)S(1)} reshape(bf16[64,2,1152]{2,1,0:T(2,128)(2,1)S(1)} %all-to-all-done.3) | data formatting | bytes 589824
  113.6 1.1 copy.172
  114.7 6.0 %copy.140 = bf16[2,36,8,64,4]{2,1,0,4,3:T(8,128)(2,1)} copy(bf16[2,36,8,64,4]{1,2,3,4,0:T(8,128)(2,1)} %bitcast.58) | data formatting | bytes 589824 | tf_op jit(solution)/shard_map/all_to_all | solution.py:112
  120.6 0.0 copy-start.2
  120.7 6.0 %reshape.185 = bf16[576,256]{0,1:T(8,128)(2,1)S(1)} reshape(bf16[2,36,8,64,4]{2,1,0,4,3:T(8,128)(2,1)} %copy.140) | data formatting | bytes 589824 | tf_op jit(solution)/shard_map/reshape | solution.py:115
  126.6 0.0 copy-done.2
  126.6 1.9 %multiply_convert_fusion = bf16[576,1440]{1,0:T(8,128)(2,1)} fusion(bf16[576,256]{0,1:T(8,128)(2,1)S(1)} %reshape.185, bf16[1440,256]{0,1:T(8,128)(2,1)S(1)} %copy-done.2), kind=kOutput, calls=%fused_computation.7 | convolution fusion | flops 426332160 | bytes 2691072 | tf_op jit(solution)/shard_map/dot_general | solution.py:114
  (4 shorter events, 0.1 us)
Async XLA Ops:
  0.6 5.8 %copy-start = (bf16[2,36,8,1440]{3,2,1,0:T(8,128)(2,1)S(1)}, bf16[2,36,8,1440]{3,2,1,0:T(8,128)(2,1)}, u32[]{:S(2)}) copy-start(bf16[2,36,8,1440]{3,2,1,0:T(8,128)(2,1)} %param.4) | copy-start | bytes 4976644
  6.4 0.9 copy-start.1
  11.6 29.5 %all-to-all-start = ((bf16[64,2,1152]{2,1,0:T(2,128)(2,1)}), bf16[64,2,1152]{2,1,0:T(2,128)(2,1)S(1)}, u32[]{:S(2)}, u32[]{:S(2)}) async-start(bf16[64,2,1152]{2,1,0:T(2,128)(2,1)} %reshape.195), calls=%async_computation | async-start | bytes 589824 | tf_op jit(solution)/shard_map/all_to_all | solution.py:59
  44.1 9.0 %copy-start.3 = (s32[128]{0:T(128)S(1)}, s32[128]{0:T(128)}, u32[]{:S(2)}) copy-start(s32[128]{0:T(128)} %param.7) | copy-start | bytes 1540
  47.5 13.7 %all-to-all-start.1 = ((bf16[2,36,512,4]{2,3,0,1:T(4,128)(2,1)}), bf16[2,36,512,4]{2,3,0,1:T(4,128)(2,1)S(1)}, u32[]{:S(2)}, u32[]{:S(2)}) async-start(bf16[2,36,512,4]{2,3,0,1:T(4,128)(2,1)} %copy.127), calls=%async_computation.1 | async-start | bytes 589824 | tf_op jit(solution)/shard_map/all_to_all | solution.py:62
  70.1 1.4 %copy-start.4 = (bf16[2,512,721]{1,0,2:T(2,128)(2,1)S(1)}, bf16[2,512,721]{1,0,2:T(2,128)(2,1)}, u32[]{:S(2)}) copy-start(bf16[2,512,721]{1,0,2:T(2,128)(2,1)} %param.6) | copy-start | bytes 4429828
  71.5 6.0 %copy-start.5 = (u32[256]{0:T(256)S(1)}, u32[256]{0:T(256)}, u32[]{:S(2)}) copy-start(u32[256]{0:T(256)} %constant.70) | copy-start | bytes 3076
  72.8 12.6 %all-to-all-start.2 = ((bf16[8,9,512,4]{2,3,1,0:T(4,128)(2,1)}), bf16[8,9,512,4]{2,3,1,0:T(4,128)(2,1)S(1)}, u32[]{:S(2)}, u32[]{:S(2)}) async-start(bf16[8,9,512,4]{2,3,1,0:T(4,128)(2,1)} %copy.136), calls=%async_computation.2 | async-start | bytes 589824 | tf_op jit(solution)/shard_map/all_to_all | solution.py:111
  89.6 21.1 %all-to-all-start.3 = ((bf16[64,2,1152]{2,1,0:T(2,128)(2,1)}), bf16[64,2,1152]{2,1,0:T(2,128)(2,1)S(1)}, u32[]{:S(2)}, u32[]{:S(2)}) async-start(bf16[64,2,1152]{2,1,0:T(2,128)(2,1)} %reshape.197), calls=%async_computation.3 | async-start | bytes 589824 | tf_op jit(solution)/shard_map/all_to_all | solution.py:112
  120.6 6.0 %copy-start.2 = (bf16[1440,256]{0,1:T(8,128)(2,1)S(1)}, bf16[1440,256]{0,1:T(8,128)(2,1)}, u32[]{:S(2)}) copy-start(bf16[1440,256]{0,1:T(8,128)(2,1)} %copy-done.1) | copy-start | bytes 2211844
where the time goes:
time: 129 us; the launch traced here: 128 us
  local copies, waits for them, and re-layouts  36.9 us (29%)
  starting transfers between devices  32.3 us (25%)
  waiting for transfers between devices  29.5 us (23%)
  other arithmetic  12 us (9%)
  blocking collectives  11.2 us (9%)
  matrix products  4.92 us (4%)
  between operations  1.55 us (1%)
    all_to_all x1, starting transfers between devices, body(): lax.all_to_all(sphere_coefficient_sets, 'lat', split_axis=3, concat_axis=...  15.6 us
    unnamed x19, local copies, waits for them, and re-layouts  14.4 us
    all_to_all x1, waiting for transfers between devices, body(): lax.all_to_all(sphere_coefficient_sets, 'lat', split_axis=3, concat_axis=...  13.9 us
    unnamed x1, blocking collectives  11.2 us
    all_to_all x2, local copies, waits for them, and re-layouts, body(): lax.all_to_all(returned, 'lat', split_axis=2, concat_axis=3, tiled=True)  7.06 us
    all_to_all x1, waiting for transfers between devices, body(): lax.all_to_all(sphere_coefficient_sets, 'ens', split_axis=1, concat_axis=...  7.03 us
    all_to_all x1, waiting for transfers between devices, body(): lax.all_to_all(returned, 'ens', split_axis=0, concat_axis=1, tiled=True)  6.66 us
    all_to_all x1, starting transfers between devices, body(): lax.all_to_all(returned, 'lat', split_axis=2, concat_axis=3, tiled=True)  6.56 us
  transfers between devices with their start and end apart: 4, of which 4 were waited for; matrix products, arithmetic and copies ran while one was open for 2% of the time, Pallas kernels for 0%

commit v1 on v0

v1 whole, which is shorter than its diff:
```python
import functools
import math

import jax
import jax.numpy as jnp
from jax import lax
from jax.experimental import pallas as pl
from jax.experimental.pallas import tpu as pltpu
from jax.sharding import PartitionSpec as P

SMOOTH = 0.1
LANES = 128
VROWS = 40
WIDTH = 768
MEMBERS = 8
F32 = jnp.float32
BF16 = jnp.bfloat16
VMEM = pltpu.VMEM
MESH_AXES = ("ens", "lat")


def dot(a, b, dims):
    return lax.dot_general(a, b, (dims, ((), ())), preferred_element_type=F32)


def fourier_kernel(lat, z_ref, x_ref, send_ref, table_ref, x_vmem, sems):
    rows, nodes = x_vmem.shape
    chunks = [(a, min(256, rows - a)) for a in range(0, rows, 256)]
    copies = [
        pltpu.make_async_copy(x_ref.at[pl.ds(a, n)], x_vmem.at[pl.ds(a, n)], sems.at[c])
        for c, (a, n) in enumerate(chunks)
    ]
    for copy in copies:
        copy.start()
    count = send_ref.shape[0]
    waves = z_ref.shape[1]
    d = lax.broadcasted_iota(jnp.int32, (count, waves), 0)
    s = lax.broadcasted_iota(jnp.int32, (count, waves), 1)
    wanted = 2 * lax.rem(d, lat) + lax.div(d, 2 * lat)
    z = jnp.sum(jnp.where(s == wanted, z_ref[...].astype(F32), 0.0), axis=1, keepdims=True)
    dcol = lax.broadcasted_iota(jnp.int32, (count, 1), 0)
    shift = (lax.rem(lax.div(dcol, lat), 2) * (nodes // 4)).astype(F32)
    j = lax.broadcasted_iota(jnp.int32, (1, nodes), 1).astype(F32)
    step = 2.0 * math.pi / nodes
    for a in range(0, count, 32):
        p = j * z[a : a + 32] + shift[a : a + 32]
        p = p - nodes * jnp.floor(p * (1.0 / nodes))
        w = (jnp.abs(p - nodes / 2) - nodes / 4) * step
        w2 = w * w
        poly = -2.5052108e-08
        for c in (2.7557319e-06, -1.9841270e-04, 8.3333333e-03, -1.6666667e-01):
            poly = poly * w2 + c
        table_ref[a : a + 32, :] = (w + w * (w2 * poly)).astype(BF16)
    scale = nodes**-0.5
    for copy, (a, n) in zip(copies, chunks):
        copy.wait()
        spectra = dot(table_ref[...], x_vmem[a : a + n, :], ((1,), (1,))) * scale
        send_ref[:, a : a + n] = spectra.astype(BF16)
    send_ref[:, rows:] = jnp.zeros((count, send_ref.shape[1] - rows), BF16)


def crps_kernel(
    lat, ens, degrees, variables,
    z_ref, recv_ref, obs_ref, pk_ref, pl_ref, send_ref,
    turned, spectra, coeffs, grads, back, pk_vmem, pl_vmem, sems,
):
    first = pltpu.make_async_copy(pk_ref, pk_vmem, sems.at[0])
    second = pltpu.make_async_copy(pl_ref, pl_vmem, sems.at[1])
    first.start()
    second.start()
    local = MEMBERS // ens
    span = variables * 8
    pairs = ens // 2
    for k2 in range(pairs):
        rows = recv_ref[k2 * LANES : (k2 + 1) * LANES, : turned.shape[1]]
        turned[k2] = rows.astype(F32).T
    low = lax.broadcasted_iota(jnp.int32, (VROWS, LANES), 1) < lat
    for t2 in range(4):
        for m in range(local):
            for k2 in range(pairs):
                even = turned[k2, pl.ds(m * span + 2 * t2, VROWS, stride=8), :]
                odd = turned[k2, pl.ds(m * span + 2 * t2 + 1, VROWS, stride=8), :]
                into = pl.ds(t2 * LANES, LANES)
                e = 2 * k2 * local + m
                spectra[pl.ds(e * VROWS, VROWS), into] = jnp.where(low, even, pltpu.roll(odd, lat, 1))
                e = e + local
                spectra[pl.ds(e * VROWS, VROWS), into] = jnp.where(low, pltpu.roll(even, lat, 1), odd)
    first.wait()
    coeffs[...] = dot(spectra[...].astype(BF16), pk_vmem[...], ((1,), (0,)))

    zonal = z_ref[0]
    factor = jnp.where(zonal == 0, 1.0, 2.0).astype(F32)
    tiles = VROWS // 8

    def one_block(b, totals):
        lanes = pl.ds(pl.multiple_of(b * LANES, LANES), LANES)
        degree = b * LANES + lax.broadcasted_iota(jnp.int32, (8, LANES), 1)
        weight = jnp.where((degree >= zonal) & (degree < degrees), factor, 0.0)
        sums = []
        for tile in range(tiles):
            c = [coeffs[pl.ds(e * VROWS + tile * 8, 8), lanes] for e in range(MEMBERS)]
            seen = obs_ref[pl.ds(tile * 8, 8), lanes]
            slope = [None] * MEMBERS
            spread = None
            for e in range(MEMBERS - 1):
                part = None
                for f in range(e + 1, MEMBERS):
                    gap = c[e] - c[f]
                    square = gap * gap + SMOOTH * SMOOTH
                    inverse = lax.rsqrt(square)
                    sign = gap * inverse
                    root = square * inverse
                    part = root if part is None else part + root
                    slope[e] = sign if slope[e] is None else slope[e] + sign
                    slope[f] = -sign if slope[f] is None else slope[f] - sign
                part = part - SMOOTH * (MEMBERS - 1 - e)
                spread = part if spread is None else spread + part
            miss = None
            for e in range(MEMBERS):
                gap = c[e] - seen
                square = gap * gap + SMOOTH * SMOOTH
                inverse = lax.rsqrt(square)
                root = square * inverse
                miss = root if miss is None else miss + root
                grad = weight * (gap * inverse * (1 / MEMBERS) - slope[e] * (1 / MEMBERS**2))
                grads[pl.ds(e * VROWS + tile * 8, 8), lanes] = grad.astype(BF16)
            miss = miss - SMOOTH * MEMBERS
            score = miss * (1 / MEMBERS) - spread * (1 / MEMBERS**2)
            sums.append(totals[tile] + weight * score)
        return tuple(sums)

    blocks = coeffs.shape[1] // LANES
    zero = jnp.zeros((8, LANES), F32)
    totals = lax.fori_loop(0, blocks, one_block, (zero,) * tiles)

    second.wait()
    returned = dot(grads[...], pl_vmem[...], ((1,), (0,)))
    for m in range(local):
        for t2 in range(4):
            for k2 in range(pairs):
                e = 2 * k2 * local + m
                even = returned[e * VROWS : (e + 1) * VROWS, t2 * LANES : (t2 + 1) * LANES]
                e = e + local
                odd = returned[e * VROWS : (e + 1) * VROWS, t2 * LANES : (t2 + 1) * LANES]
                row = m * span + 2 * t2
                back[k2, pl.ds(row, VROWS, stride=8), :] = jnp.where(low, even, pltpu.roll(odd, lat, 1))
                back[k2, pl.ds(row + 1, VROWS, stride=8), :] = jnp.where(low, pltpu.roll(even, lat, 1), odd)
    base = back.shape[1] - LANES
    for tile in range(tiles):
        rest = jnp.sum(totals[tile], axis=1, keepdims=True) * (1.0 / degrees)
        for term in range(3):
            piece = rest.astype(BF16).astype(F32)
            rest = rest - piece
            for k2 in range(pairs):
                spot = pl.ds(base + term * VROWS + tile * 8, 8)
                back[k2, spot, :] = jnp.broadcast_to(piece, (8, LANES))
    for k2 in range(pairs):
        back[k2, base + 3 * VROWS :, :] = jnp.zeros((LANES - 3 * VROWS, LANES), F32)
        send_ref[k2 * LANES : (k2 + 1) * LANES, :] = back[k2].T.astype(BF16)


def grid_kernel(lat, ens, variables, at_ref, recv_ref, table_ref, out_ref, score_ref, block, sems):
    rows, nodes = out_ref.shape
    scale = nodes**-0.5
    copies = []
    for c, a in enumerate(range(0, rows, LANES)):
        n = min(LANES, rows - a)
        part = dot(recv_ref[:, a : a + n], table_ref[...], ((0,), (0,))) * scale
        block[a : a + n, :] = part.astype(BF16)
        copy = pltpu.make_async_copy(block.at[pl.ds(a, n)], out_ref.at[pl.ds(a, n)], sems.at[c])
        copy.start()
        copies.append(copy)
    base = recv_ref.shape[1] - LANES
    mine = lax.broadcasted_iota(jnp.int32, (lat, LANES), 0) == at_ref[0]
    for k in range(ens):
        terms = recv_ref[k * lat : (k + 1) * lat, base : base + LANES].astype(F32)
        terms = jnp.sum(jnp.where(mine, terms, 0.0), axis=0, keepdims=True)
        total = terms + pltpu.roll(terms, LANES - VROWS, 1) + pltpu.roll(terms, LANES - 2 * VROWS, 1)
        score_ref[k % 2, k // 2 : k // 2 + 1, :] = total[:, :variables]
    for copy in copies:
        copy.wait()


def exchange(values):
    count, width = values.shape
    values = values.reshape(count, 2, width // 2)
    values = lax.all_to_all(values, MESH_AXES, 0, 0, tiled=True)
    return values.reshape(count, width)


def body(predicted_grid, verifying_coefficients, weighted_polynomial_values, zonal_order_values):
    local, variables, lines, nodes = predicted_grid.shape
    _, all_lines, degrees = weighted_polynomial_values.shape
    lat = lax.axis_size("lat")
    ens = lax.axis_size("ens")
    count = lat * ens
    rows = local * variables * lines
    padded = -(-degrees // LANES) * LANES
    whole = pl.BlockSpec(memory_space=VMEM)
    scalar = pl.BlockSpec(memory_space=pltpu.SMEM)
    anywhere = pl.BlockSpec(memory_space=pl.ANY)
    at_lat = lax.axis_index("lat")
    at_ens = lax.axis_index("ens")
    slot = at_ens // 2
    part = at_ens % 2

    send, table = pl.pallas_call(
        functools.partial(fourier_kernel, lat),
        name="fourier",
        in_specs=[whole, anywhere],
        out_specs=[whole, whole],
        out_shape=[
            jax.ShapeDtypeStruct((count, WIDTH), BF16),
            jax.ShapeDtypeStruct((count, nodes), BF16),
        ],
        scratch_shapes=[VMEM((rows, nodes), BF16), pltpu.SemaphoreType.DMA((3,))],
    )(zonal_order_values.reshape(1, -1), predicted_grid.reshape(rows, nodes))
    recv = exchange(send)

    basis = lax.dynamic_index_in_dim(weighted_polynomial_values, slot, 0, False)
    basis = basis.reshape(lat, lines, degrees).transpose(1, 0, 2).reshape(all_lines, degrees)
    basis = jnp.pad(basis, ((0, 0), (0, padded - degrees)))
    observed = lax.dynamic_index_in_dim(verifying_coefficients, part, 1, False)
    observed = lax.dynamic_index_in_dim(observed, slot, 1, False)
    observed = jnp.pad(observed, ((0, VROWS - variables), (0, padded - degrees)))
    own_wave = lax.dynamic_slice_in_dim(zonal_order_values, 2 * at_lat + slot, 1)

    send = pl.pallas_call(
        functools.partial(crps_kernel, lat, ens, degrees, variables),
        name="crps",
        in_specs=[scalar, whole, whole, anywhere, anywhere],
        out_specs=whole,
        out_shape=jax.ShapeDtypeStruct((count, WIDTH), BF16),
        scratch_shapes=[
            VMEM((ens // 2, 5 * LANES, LANES), F32),
            VMEM((MEMBERS * VROWS, all_lines), F32),
            VMEM((MEMBERS * VROWS, padded), F32),
            VMEM((MEMBERS * VROWS, padded), BF16),
            VMEM((ens // 2, WIDTH, LANES), F32),
            VMEM((all_lines, padded), BF16),
            VMEM((padded, all_lines), BF16),
            pltpu.SemaphoreType.DMA((2,)),
        ],
    )(own_wave, recv, observed, basis, basis.T)
    recv = exchange(send)

    sensitivity, scores = pl.pallas_call(
        functools.partial(grid_kernel, lat, ens, variables),
        name="grid",
        in_specs=[scalar, whole, whole],
        out_specs=[anywhere, whole],
        out_shape=[
            jax.ShapeDtypeStruct((rows, nodes), BF16),
            jax.ShapeDtypeStruct((2, 2, variables), F32),
        ],
        scratch_shapes=[VMEM((rows, nodes), BF16), pltpu.SemaphoreType.DMA((5,))],
    )(at_lat.reshape(1), recv, table)
    return sensitivity.reshape(predicted_grid.shape), scores.transpose(2, 0, 1)


def solution(mesh):
    placed = (P("ens", None, "lat", None), P(None, None, "lat", None), P("lat", None, None), P())
    return jax.shard_map(
        body,
        mesh=mesh,
        in_specs=placed,
        out_specs=(P("ens", None, "lat", None), P(None, None, "lat")),
        check_vma=False,
    )
```

time: 129 us -> 78.2 us (0.61)
  local copies, waits for them, and re-layouts: 36.9 us -> 15.1 us
  waiting for transfers between devices: 29.5 us -> 7.94 us
  starting transfers between devices: 32.3 us -> 15.6 us
  Pallas kernels: 0 us -> 14.2 us
  blocking collectives: 11.2 us -> 24.2 us
  other arithmetic: 12 us -> 0 us
  matrix products: 4.92 us -> 0 us
    all_to_all x0 -> x1, blocking collectives: none -> 24.2 us  [exchange(): values = lax.all_to_all(values, MESH_AXES, 0, 0, tiled=True)]
    all_to_all x4 -> x1, waiting for transfers between devices: 29.5 us -> 7.94 us  [exchange(): values = lax.all_to_all(values, MESH_AXES, 0, 0, tiled=True)]
    all_to_all x4 -> x1, starting transfers between devices: 32.3 us -> 15.6 us  [exchange(): values = lax.all_to_all(values, MESH_AXES, 0, 0, tiled=True)]
    pallas_call x0 -> x3, Pallas kernels: none -> 14.2 us  [the longest x1 6.25 us: body(): pl.pallas_call(functools.partial(crps_kernel, lat, ens, degrees, variable...]
    all_to_all x7 -> x0, local copies, waits for them, and re-layouts: 11.6 us -> none  [the longest x2 7.06 us: body(): lax.all_to_all(returned, 'lat', split_axis=2, concat_axis=3, tiled=True)]
    unnamed x1 -> x0, blocking collectives: 11.2 us -> none
    unnamed x19 -> x9, local copies, waits for them, and re-layouts: 14.4 us -> 4.95 us
    reduce_sum x3 -> x0, other arithmetic: 7.5 us -> none  [the longest x1 6.53 us: body(): jnp.sum(spread_abs, axis=1) / (2 * realization_pile * realization_pile)]
  transfers between devices with their start and end apart: 4 -> 1, of which waited for: 4 -> 1; matrix products, arithmetic and copies ran while one was open for 2% -> 14% of each run, Pallas kernels for 0% -> 0%
where the time goes in v1:
time: 78.2 us; the launch traced here: 77.9 us
  blocking collectives  24.2 us (31%)
  starting transfers between devices  15.6 us (20%)
  local copies, waits for them, and re-layouts  15.1 us (19%)
  Pallas kernels  14.2 us (18%)
  waiting for transfers between devices  7.94 us (10%)
    all_to_all x1, blocking collectives, exchange(): values = lax.all_to_all(values, MESH_AXES, 0, 0, tiled=True)  24.2 us
    all_to_all x1, starting transfers between devices, exchange(): values = lax.all_to_all(values, MESH_AXES, 0, 0, tiled=True)  15.6 us
    all_to_all x1, waiting for transfers between devices, exchange(): values = lax.all_to_all(values, MESH_AXES, 0, 0, tiled=True)  7.94 us
    pallas_call x1, Pallas kernels, body(): pl.pallas_call(functools.partial(crps_kernel, lat, ens, degrees, variable...  6.25 us
    unnamed x9, local copies, waits for them, and re-layouts  4.95 us
    pallas_call x1, Pallas kernels, body(): pl.pallas_call(functools.partial(fourier_kernel, lat), name='fourier', in...  4.55 us
    pallas_call x1, Pallas kernels, body(): pl.pallas_call(functools.partial(grid_kernel, lat, ens, variables), name=...  3.37 us
    reshape x2, local copies, waits for them, and re-layouts, exchange(): values = values.reshape(count, 2, width // 2)  2.93 us
  transfers between devices with their start and end apart: 1, of which 1 were waited for; matrix products, arithmetic and copies ran while one was open for 14% of the time, Pallas kernels for 0%

profile of v1, /device:TPU:1, one launch (start us, length us, event | category | flops | bytes accessed | tf_op | source)
XLA Modules:
  0.0 77.9 jit_solution(14041109925029243830)
XLA Ops:
  0.6 0.0 copy-start
  0.6 4.5 %fourier.1 = (bf16[256,768]{1,0:T(8,128)(2,1)}, bf16[256,1440]{1,0:T(8,128)(2,1)}) custom-call(s32[1,128]{1,0:T(1,128)} %bitcast.26, bf16[576,1440]{1,0:T(8,128)(2,1)} %bitcast.20), custom_call_target="tpu_custom_call" | custom-call | tf_op jit(solution)/shard_map/fourier/pallas_call | solution.py:207
  5.2 1.8 %reshape.40 = bf16[256,2,384]{2,1,0:T(2,128)(2,1)} reshape(bf16[256,768]{1,0:T(8,128)(2,1)} %get-tuple-element.6) | data formatting | bytes 786432 | tf_op jit(solution)/shard_map/reshape | solution.py:186
  7.0 15.6 %all-to-all-start = ((bf16[256,2,384]{2,1,0:T(2,128)(2,1)}), bf16[256,2,384]{2,1,0:T(2,128)(2,1)S(1)}, u32[]{:S(2)}, u32[]{:S(2)}) async-start(bf16[256,2,384]{2,1,0:T(2,128)(2,1)} %reshape.40), calls=%async_computation | async-start | bytes 786432 | tf_op jit(solution)/shard_map/all_to_all | solution.py:187
  22.7 0.0 copy-done
  22.7 1.5 %constant_dynamic-slice_fusion = bf16[1,512,721]{1,0,2:T(2,128)(2,1)S(1)} fusion(bf16[2,512,721]{1,0,2:T(2,128)(2,1)S(1)} %copy-done, s32[]{:T(128)S(6)} %select_n.33), kind=kLoop, calls=%fused_computation.1 | loop fusion | bytes 1476612 | tf_op jit(solution)/shard_map/jit(dynamic_index_in_dim)/dynamic_slice | solution.py:220
  24.3 3.0 %copy.13 = bf16[1,512,721]{2,1,0:T(8,128)(2,1)} copy(bf16[1,512,721]{1,0,2:T(2,128)(2,1)S(1)} %constant_dynamic-slice_fusion) | data formatting | bytes 1476608
  27.3 1.3 %copy.9 = bf16[8,64,721]{2,1,0:T(8,128)(2,1)S(1)} copy(bf16[8,64,721]{2,0,1:T(8,128)(2,1)} %bitcast.18) | data formatting | bytes 1476608 | tf_op jit(solution)/shard_map/transpose | solution.py:221
  28.6 0.0 copy-start.1
  28.6 0.3 copy.10
  28.9 0.3 copy.17
  29.2 1.0 %constant_dynamic-slice_fusion.1 = f32[36,1,1,721]{3,2,1,0:T(1,128)S(1)} fusion(f32[36,2,2,721]{3,2,1,0:T(2,128)} %param.5, s32[]{:T(128)S(6)} %select_n.32, s32[]{:T(128)S(6)} %select_n.34), kind=kLoop, calls=%fused_computation.2 | loop fusion | bytes 207656 | tf_op jit(solution)/shard_map/jit(dynamic_index_in_dim)/dynamic_slice | solution.py:224
  30.2 0.0 copy-done.1
  30.2 0.6 dynamic_slice.13.z_ref
  30.8 0.9 %pad.9.clone.pk_ref = bf16[512,768]{1,0:T(8,128)(2,1)} pad(bf16[512,721]{1,0:T(8,128)(2,1)S(1)} %copy.17, bf16[]{:T(256)} %constant.71.clone.1), padding=0_0x0_47 | pad | bytes 1524738 | tf_op jit(solution)/shard_map/jit(_pad)/pad | solution.py:222
  31.8 0.7 pad.8.obs_ref
  32.4 0.9 %pad_bitcast_fusion.pl_ref = bf16[768,512]{1,0:T(8,128)(2,1)} fusion(bf16[512,721]{0,1:T(8,128)(2,1)S(1)} %copy.10), kind=kLoop, calls=%fused_computation.3 | loop fusion | bytes 1524736 | tf_op jit(solution)/shard_map/transpose | solution.py:244
  33.4 7.9 %all-to-all-done = bf16[256,2,384]{2,1,0:T(2,128)(2,1)S(1)} async-done(((bf16[256,2,384]{2,1,0:T(2,128)(2,1)}), bf16[256,2,384]{2,1,0:T(2,128)(2,1)S(1)}, u32[]{:S(2)}, u32[]{:S(2)}) %all-to-all-start) | async-done | bytes 393248 | tf_op jit(solution)/shard_map/all_to_all | solution.py:187
  41.3 0.8 %copy.14 = bf16[32,8,2,384]{3,1,2,0:T(8,128)(2,1)} copy(bf16[32,8,2,384]{3,2,1,0:T(2,128)(2,1)S(1)} %bitcast.21) | data formatting | bytes 786432
  42.1 6.3 %crps.1 = bf16[256,768]{1,0:T(8,128)(2,1)} custom-call(s32[1]{0:T(128)} %dynamic_slice.13.z_ref, bf16[256,768]{1,0:T(8,128)(2,1)} %bitcast.24, f32[40,768]{1,0:T(8,128)} %pad.8.obs_ref, bf16[512,768]{1,0:T(8,128)(2,1)} %pad.9.clone.pk_ref, bf16[768,512]{1,0:T(8,128)(2,1)} %pad_bitcast_fusion.pl_ref), custom_call_target="tpu_custom_call" | custom-call | tf_op jit(solution)/shard_map/crps/pallas_call | solution.py:228
  48.4 1.1 %reshape.44 = bf16[256,2,384]{2,1,0:T(2,128)(2,1)S(1)} reshape(bf16[256,768]{1,0:T(8,128)(2,1)} %crps.1) | data formatting | bytes 786432 | tf_op jit(solution)/shard_map/reshape | solution.py:186
  49.5 24.2 %all_to_all.10 = bf16[256,2,384]{2,1,0:T(2,128)(2,1)S(1)} all-to-all(bf16[256,2,384]{2,1,0:T(2,128)(2,1)S(1)} %reshape.44), channel_id=1, replica_groups=mesh['lat'=64,'ens'=4] {'ens','lat'}, dimensions={0} | all-to-all | bytes 786432 | tf_op jit(solution)/shard_map/all_to_all | solution.py:187
  73.7 0.8 %copy.15 = bf16[32,8,2,384]{3,1,2,0:T(8,128)(2,1)} copy(bf16[32,8,2,384]{3,2,1,0:T(2,128)(2,1)S(1)} %bitcast.22) | data formatting | bytes 786432
  74.5 3.4 %grid.1 = (bf16[576,1440]{1,0:T(8,128)(2,1)}, f32[2,2,36]{2,1,0:T(2,128)}) custom-call(s32[1]{0:T(128)} %bitcast.at_ref, bf16[256,768]{1,0:T(8,128)(2,1)} %bitcast.23, bf16[256,1440]{1,0:T(8,128)(2,1)} %get-tuple-element.7.table_ref), custom_call_target="tpu_custom_call" | custom-call | tf_op jit(solution)/shard_map/grid/pallas_call | solution.py:247
  (1 shorter events, 0.0 us)
Async XLA Ops:
  0.6 22.1 %copy-start = (bf16[2,512,721]{1,0,2:T(2,128)(2,1)S(1)}, bf16[2,512,721]{1,0,2:T(2,128)(2,1)}, u32[]{:S(2)}) copy-start(bf16[2,512,721]{1,0,2:T(2,128)(2,1)} %param.6) | copy-start | bytes 4429828
  7.0 34.3 %all-to-all-start = ((bf16[256,2,384]{2,1,0:T(2,128)(2,1)}), bf16[256,2,384]{2,1,0:T(2,128)(2,1)S(1)}, u32[]{:S(2)}, u32[]{:S(2)}) async-start(bf16[256,2,384]{2,1,0:T(2,128)(2,1)} %reshape.40), calls=%async_computation | async-start | bytes 786432 | tf_op jit(solution)/shard_map/all_to_all | solution.py:187
  28.6 1.7 %copy-start.1 = (s32[128]{0:T(128)S(1)}, s32[128]{0:T(128)}, u32[]{:S(2)}) copy-start(s32[128]{0:T(128)} %param.7) | copy-start | bytes 1540

commit v2 on v1

v2 whole, which is shorter than its diff:
```python
import functools
import math

import jax
import jax.numpy as jnp
from jax import lax
from jax.experimental import pallas as pl
from jax.experimental.pallas import tpu as pltpu
from jax.sharding import PartitionSpec as P

SMOOTH = 0.1
LANES = 128
VROWS = 40
WIDTH = 384
MEMBERS = 8
F32 = jnp.float32
BF16 = jnp.bfloat16
VMEM = pltpu.VMEM
PARAMS = pltpu.CompilerParams(vmem_limit_bytes=16 * 1024 * 1024)
MESH_AXES = ("ens", "lat")


def dot(a, b, dims):
    return lax.dot_general(a, b, (dims, ((), ())), preferred_element_type=F32)


def fourier_kernel(lat, z_far, x_ref, send_ref, table_far, z_ref, x_vmem, table_ref, sems):
    local, width, nodes = x_vmem.shape
    span = x_ref.shape[1]
    copies = [
        pltpu.make_async_copy(x_ref.at[m], x_vmem.at[m, pl.ds(0, span)], sems.at[m]) for m in range(local)
    ]
    waves = pltpu.make_async_copy(z_far, z_ref, sems.at[local + 1])
    waves.start()
    for copy in copies:
        copy.start()
    for m in range(local):
        x_vmem[m, span:, :] = jnp.zeros((width - span, nodes), BF16)
    count = send_ref.shape[0]
    shape = (count, z_ref.shape[1])
    d = lax.broadcasted_iota(jnp.int32, shape, 0)
    s = lax.broadcasted_iota(jnp.int32, shape, 1)
    wanted = 2 * lax.rem(d, lat) + lax.div(d, 2 * lat)
    waves.wait()
    z = jnp.sum(jnp.where(s == wanted, z_ref[...].astype(F32), 0.0), axis=1, keepdims=True)
    dcol = lax.broadcasted_iota(jnp.int32, (count, 1), 0)
    shift = (lax.rem(lax.div(dcol, lat), 2) * (nodes // 4)).astype(F32)
    j = lax.broadcasted_iota(jnp.int32, (1, nodes), 1).astype(F32)
    step = 2.0 * math.pi / nodes
    for a in range(0, count, 32):
        p = j * z[a : a + 32] + shift[a : a + 32]
        p = p - nodes * jnp.floor(p * (1.0 / nodes))
        w = (jnp.abs(p - nodes / 2) - nodes / 4) * step
        w2 = w * w
        poly = -2.5052108e-08
        for c in (2.7557319e-06, -1.9841270e-04, 8.3333333e-03, -1.6666667e-01):
            poly = poly * w2 + c
        table_ref[a : a + 32, :] = (w + w * (w2 * poly)).astype(BF16)
    scale = nodes**-0.5
    keep = pltpu.make_async_copy(table_ref, table_far, sems.at[local])
    keep.start()
    for m, copy in enumerate(copies):
        copy.wait()
        spectra = dot(table_ref[...], x_vmem[m], ((1,), (1,))) * scale
        send_ref[:, m, :] = spectra.astype(BF16)
    keep.wait()


def basis_kernel(lat, where_ref, p_ref, v_ref, pk_ref, pl_ref, obs_ref, p_vmem, v_vmem, mine, sems):
    slot = where_ref[0]
    first = pltpu.make_async_copy(p_ref, p_vmem, sems.at[0])
    second = pltpu.make_async_copy(v_ref.at[:, where_ref[1]], v_vmem, sems.at[1])
    first.start()
    second.start()
    degrees, _, lines = p_vmem.shape
    first.wait()
    step = 16

    def pick(start, size):
        both = p_vmem[pl.ds(start, size)].astype(F32)
        chosen = jnp.where(slot == 0, both[:, 0, :], both[:, 1, :])
        mine[pl.ds(start, size), :] = chosen.astype(BF16)

    def one(i, carry):
        pick(pl.multiple_of(i * step, step), step)
        return carry

    lax.fori_loop(0, degrees // step, one, 0)
    rest = degrees % step
    if rest:
        pick(degrees - rest, rest)
    rows = lines // lat
    source = lax.broadcasted_iota(jnp.int32, (lines, lines), 0)
    target = lax.broadcasted_iota(jnp.int32, (lines, lines), 1)
    order = source == rows * lax.rem(target, lat) + lax.div(target, lat)
    turned = dot(mine[...], order.astype(F32).astype(BF16), ((1,), (0,)))
    pl_ref[...] = turned.astype(BF16)
    pk_ref[...] = turned.T.astype(BF16)
    second.wait()
    seen = v_vmem[...]
    obs_ref[...] = jnp.zeros(obs_ref.shape, F32)
    obs_ref[: seen.shape[0], :degrees] = jnp.where(slot == 0, seen[:, 0, :], seen[:, 1, :])


def crps_kernel(
    lat, ens, degrees, variables,
    z_ref, recv_ref, obs_far, pk_far, pl_far, send_ref,
    turned, spectra, coeffs, grads, back, obs_ref, pk_ref, pl_ref, sems,
):
    copies = [
        pltpu.make_async_copy(far, near, sems.at[c])
        for c, (far, near) in enumerate(((pk_far, pk_ref), (obs_far, obs_ref), (pl_far, pl_ref)))
    ]
    for copy in copies:
        copy.start()
    local = MEMBERS // ens
    pairs = ens // 2
    for m in range(local):
        for k2 in range(pairs):
            rows = recv_ref[k2 * LANES : (k2 + 1) * LANES, m, :]
            turned[m, k2] = rows.astype(F32).T
    low = lax.broadcasted_iota(jnp.int32, (VROWS, LANES), 1) < lat
    for t2 in range(4):
        for m in range(local):
            for k2 in range(pairs):
                even = turned[m, k2, pl.ds(2 * t2, VROWS, stride=8), :]
                odd = turned[m, k2, pl.ds(2 * t2 + 1, VROWS, stride=8), :]
                into = pl.ds(t2 * LANES, LANES)
                e = 2 * k2 * local + m
                spectra[pl.ds(e * VROWS, VROWS), into] = jnp.where(low, even, pltpu.roll(odd, lat, 1))
                e = e + local
                spectra[pl.ds(e * VROWS, VROWS), into] = jnp.where(low, pltpu.roll(even, lat, 1), odd)
    copies[0].wait()
    coeffs[:, :degrees] = dot(spectra[...].astype(BF16), pk_ref[...], ((1,), (0,)))

    copies[1].wait()
    zonal = z_ref[0]
    factor = jnp.where(zonal == 0, 1.0, 2.0).astype(F32)
    tiles = VROWS // 8

    def one_block(b, totals):
        lanes = pl.ds(pl.multiple_of(b * LANES, LANES), LANES)
        degree = b * LANES + lax.broadcasted_iota(jnp.int32, (8, LANES), 1)
        active = (degree >= zonal) & (degree < degrees)
        sums = []
        for tile in range(tiles):
            c = [coeffs[pl.ds(e * VROWS + tile * 8, 8), lanes] for e in range(MEMBERS)]
            seen = obs_ref[pl.ds(tile * 8, 8), lanes]
            slope = [None] * MEMBERS
            spread = None
            for e in range(MEMBERS - 1):
                part = None
                for f in range(e + 1, MEMBERS):
                    gap = c[e] - c[f]
                    square = gap * gap + SMOOTH * SMOOTH
                    inverse = lax.rsqrt(square)
                    sign = gap * inverse
                    root = square * inverse
                    part = root if part is None else part + root
                    slope[e] = sign if slope[e] is None else slope[e] + sign
                    slope[f] = -sign if slope[f] is None else slope[f] - sign
                part = part - SMOOTH * (MEMBERS - 1 - e)
                spread = part if spread is None else spread + part
            miss = None
            for e in range(MEMBERS):
                gap = c[e] - seen
                square = gap * gap + SMOOTH * SMOOTH
                inverse = lax.rsqrt(square)
                root = square * inverse
                miss = root if miss is None else miss + root
                grad = factor * (gap * inverse * (1 / MEMBERS) - slope[e] * (1 / MEMBERS**2))
                grad = jnp.where(active, grad, 0.0)
                grads[pl.ds(e * VROWS + tile * 8, 8), lanes] = grad.astype(BF16)
            miss = miss - SMOOTH * MEMBERS
            score = miss * (1 / MEMBERS) - spread * (1 / MEMBERS**2)
            sums.append(totals[tile] + jnp.where(active, factor * score, 0.0))
        return tuple(sums)

    blocks = coeffs.shape[1] // LANES
    zero = jnp.zeros((8, LANES), F32)
    totals = lax.fori_loop(0, blocks, one_block, (zero,) * tiles)

    copies[2].wait()
    returned = dot(grads[:, :degrees], pl_ref[...], ((1,), (0,)))
    for m in range(local):
        for t2 in range(4):
            for k2 in range(pairs):
                e = 2 * k2 * local + m
                even = returned[e * VROWS : (e + 1) * VROWS, t2 * LANES : (t2 + 1) * LANES]
                e = e + local
                odd = returned[e * VROWS : (e + 1) * VROWS, t2 * LANES : (t2 + 1) * LANES]
                row = 2 * t2
                back[m, k2, pl.ds(row, VROWS, stride=8), :] = jnp.where(low, even, pltpu.roll(odd, lat, 1))
                back[m, k2, pl.ds(row + 1, VROWS, stride=8), :] = jnp.where(low, pltpu.roll(even, lat, 1), odd)
    span = variables * 8
    for tile in range(tiles):
        rest = jnp.sum(totals[tile], axis=1, keepdims=True) * (1.0 / degrees)
        for m, at in ((0, span), (0, span + VROWS), (1, span)):
            piece = rest.astype(BF16).astype(F32)
            rest = rest - piece
            for k2 in range(pairs):
                back[m, k2, pl.ds(at + tile * 8, 8), :] = jnp.broadcast_to(piece, (8, LANES))
    for m in range(local):
        used = span + VROWS * (2 - m)
        for k2 in range(pairs):
            back[m, k2, used:, :] = jnp.zeros((WIDTH - used, LANES), F32)
            send_ref[k2 * LANES : (k2 + 1) * LANES, m, :] = back[m, k2].T.astype(BF16)


def grid_kernel(lat, ens, variables, at_ref, recv_ref, table_far, out_ref, score_ref, block, table_ref, sems):
    load = pltpu.make_async_copy(table_far, table_ref, sems.at[6])
    load.start()
    local, span, nodes = out_ref.shape
    scale = nodes**-0.5
    copies = []
    for m in range(local):
        turned = recv_ref[:, m, :].astype(F32).T.astype(BF16)
        if m == 0:
            load.wait()
        for a in range(0, span, LANES):
            n = min(LANES, span - a)
            part = dot(turned[a : a + n, :], table_ref[...], ((1,), (0,))) * scale
            block[m, a : a + n, :] = part.astype(BF16)
            copy = pltpu.make_async_copy(
                block.at[m, pl.ds(a, n)], out_ref.at[m, pl.ds(a, n)], sems.at[len(copies)]
            )
            copy.start()
            copies.append(copy)
    base = WIDTH - LANES
    mine = lax.broadcasted_iota(jnp.int32, (lat, LANES), 0) == at_ref[0]
    for k in range(ens):
        terms = [
            jnp.sum(
                jnp.where(mine, recv_ref[k * lat : (k + 1) * lat, m, base:].astype(F32), 0.0),
                axis=0, keepdims=True,
            )
            for m in range(2)
        ]
        total = terms[0] + pltpu.roll(terms[0], LANES - VROWS, 1) + terms[1]
        total = pltpu.roll(total, LANES - (span - base), 1)
        score_ref[k % 2, k // 2 : k // 2 + 1, :] = total[:, :variables]
    for copy in copies:
        copy.wait()


def far_of(*arrays):
    return [pltpu.with_memory_space_constraint(a, pltpu.HBM) for a in arrays]


def exchange(values):
    return lax.all_to_all(values, MESH_AXES, 0, 0, tiled=True)


def body(predicted_grid, verifying_coefficients, weighted_polynomial_values, zonal_order_values):
    local, variables, lines, nodes = predicted_grid.shape
    slots, all_lines, degrees = weighted_polynomial_values.shape
    lat = lax.axis_size("lat")
    ens = lax.axis_size("ens")
    count = lat * ens
    span = variables * lines
    padded = -(-degrees // LANES) * LANES
    whole = pl.BlockSpec(memory_space=VMEM)
    scalar = pl.BlockSpec(memory_space=pltpu.SMEM)
    far = pl.BlockSpec(memory_space=pltpu.HBM)
    at_lat = lax.axis_index("lat")
    at_ens = lax.axis_index("ens")
    slot = at_ens // 2
    sent = jax.ShapeDtypeStruct((count, local, WIDTH), BF16)

    send, table = pl.pallas_call(
        functools.partial(fourier_kernel, lat),
        name="fourier",
        compiler_params=PARAMS,
        in_specs=[far, far],
        out_specs=[whole, far],
        out_shape=[sent, pltpu.HBM((count, nodes), BF16)],
        scratch_shapes=[
            VMEM((1, zonal_order_values.shape[0]), jnp.int32),
            VMEM((local, WIDTH, nodes), BF16),
            VMEM((count, nodes), BF16),
            pltpu.SemaphoreType.DMA((4,)),
        ],
    )(*far_of(zonal_order_values.reshape(1, -1), predicted_grid.reshape(local, span, nodes)))
    recv = exchange(send)

    by_line, by_degree, observed = pl.pallas_call(
        functools.partial(basis_kernel, lat),
        name="basis",
        compiler_params=PARAMS,
        in_specs=[scalar, far, far],
        out_specs=[whole, whole, whole],
        out_shape=[
            pltpu.HBM((all_lines, degrees), BF16),
            pltpu.HBM((degrees, all_lines), BF16),
            pltpu.HBM((VROWS, padded), F32),
        ],
        scratch_shapes=[
            VMEM((degrees, slots, all_lines), BF16),
            VMEM((variables, slots, degrees), F32),
            VMEM((degrees, all_lines), BF16),
            pltpu.SemaphoreType.DMA((2,)),
        ],
        cost_estimate=pl.CostEstimate(flops=2 * degrees * all_lines**2, bytes_accessed=4_000_000, transcendentals=0),
    )(
        jnp.stack([slot, at_ens % 2]),
        *far_of(weighted_polynomial_values.transpose(2, 0, 1), verifying_coefficients),
    )
    own_wave = lax.dynamic_slice_in_dim(zonal_order_values, 2 * at_lat + slot, 1)

    send = pl.pallas_call(
        functools.partial(crps_kernel, lat, ens, degrees, variables),
        name="crps",
        compiler_params=PARAMS,
        in_specs=[scalar, whole, far, far, far],
        out_specs=whole,
        out_shape=sent,
        scratch_shapes=[
            VMEM((local, ens // 2, WIDTH, LANES), F32),
            VMEM((MEMBERS * VROWS, all_lines), F32),
            VMEM((MEMBERS * VROWS, padded), F32),
            VMEM((MEMBERS * VROWS, padded), BF16),
            VMEM((local, ens // 2, WIDTH, LANES), F32),
            VMEM((VROWS, padded), F32),
            VMEM((all_lines, degrees), BF16),
            VMEM((degrees, all_lines), BF16),
            pltpu.SemaphoreType.DMA((3,)),
        ],
    )(own_wave, recv, *far_of(observed, by_line, by_degree))
    recv = exchange(send)

    sensitivity, scores = pl.pallas_call(
        functools.partial(grid_kernel, lat, ens, variables),
        name="grid",
        compiler_params=PARAMS,
        in_specs=[scalar, whole, far],
        out_specs=[far, whole],
        out_shape=[
            jax.ShapeDtypeStruct((local, span, nodes), BF16),
            jax.ShapeDtypeStruct((2, 2, variables), F32),
        ],
        scratch_shapes=[
            VMEM((local, span, nodes), BF16),
            VMEM((count, nodes), BF16),
            pltpu.SemaphoreType.DMA((7,)),
        ],
    )(at_lat.reshape(1), recv, *far_of(table))
    return sensitivity.reshape(predicted_grid.shape), scores.transpose(2, 0, 1)


def solution(mesh):
    placed = (P("ens", None, "lat", None), P(None, None, "lat", None), P("lat", None, None), P())
    return jax.shard_map(
        body,
        mesh=mesh,
        in_specs=placed,
        out_specs=(P("ens", None, "lat", None), P(None, None, "lat")),
        check_vma=False,
    )
```

time: 78.2 us -> 71.8 us (0.918)
  local copies, waits for them, and re-layouts: 15.1 us -> 0.6 us
  Pallas kernels: 14.2 us -> 18.7 us
  waiting for transfers between devices: 7.94 us -> 11.9 us
    pallas_call x1 -> x2, Pallas kernels: 4.55 us -> 10.4 us  [the longest x1 6.06 us: body(): pl.pallas_call(functools.partial(basis_kernel, lat), name='basis', compil...]
    unnamed x9 -> x2, local copies, waits for them, and re-layouts: 4.95 us -> 0.01 us
    all_to_all x1, waiting for transfers between devices: 7.94 us -> 11.9 us  [exchange(): return lax.all_to_all(values, MESH_AXES, 0, 0, tiled=True)]
    reshape x3 -> x0, local copies, waits for them, and re-layouts: 3.2 us -> none  [the longest x2 2.93 us: exchange(): values = values.reshape(count, 2, width // 2)]
    dynamic_slice x2 -> x0, local copies, waits for them, and re-layouts: 2.56 us -> none  [the longest x1 1.52 us: body(): basis = lax.dynamic_index_in_dim(weighted_polynomial_values, slot, 0, False)]
    transpose x2 -> x0, local copies, waits for them, and re-layouts: 2.21 us -> none  [the longest x1 1.27 us: body(): basis.reshape(lat, lines, degrees).transpose(1, 0, 2)]
    pad x2 -> x0, local copies, waits for them, and re-layouts: 1.6 us -> none  [the longest x1 0.95 us: body(): basis = jnp.pad(basis, ((0, 0), (0, padded - degrees)))]
    pallas_call x1, Pallas kernels: 6.25 us -> 4.68 us  [body(): pl.pallas_call(functools.partial(crps_kernel, lat, ens, degrees, variable...]
  transfers between devices with their start and end apart: 1 -> 1, of which waited for: 1 -> 1; matrix products, arithmetic and copies ran while one was open for 14% -> 1% of each run, Pallas kernels for 0% -> 8%
where the time goes in v2:
time: 71.8 us; the launch traced here: 71.5 us
  blocking collectives  23.9 us (33%)
  Pallas kernels  18.7 us (26%)
  starting transfers between devices  15.7 us (22%)
  waiting for transfers between devices  11.9 us (17%)
    all_to_all x1, blocking collectives, exchange(): return lax.all_to_all(values, MESH_AXES, 0, 0, tiled=True)  23.9 us
    all_to_all x1, starting transfers between devices, exchange(): return lax.all_to_all(values, MESH_AXES, 0, 0, tiled=True)  15.7 us
    all_to_all x1, waiting for transfers between devices, exchange(): return lax.all_to_all(values, MESH_AXES, 0, 0, tiled=True)  11.9 us
    pallas_call x1, Pallas kernels, body(): pl.pallas_call(functools.partial(basis_kernel, lat), name='basis', compil...  6.06 us
    pallas_call x1, Pallas kernels, body(): pl.pallas_call(functools.partial(crps_kernel, lat, ens, degrees, variable...  4.68 us
    pallas_call x1, Pallas kernels, body(): pl.pallas_call(functools.partial(fourier_kernel, lat), name='fourier', co...  4.33 us
    pallas_call x1, Pallas kernels, body(): pl.pallas_call(functools.partial(grid_kernel, lat, ens, variables), name=...  3.63 us
  transfers between devices with their start and end apart: 1, of which 1 were waited for; matrix products, arithmetic and copies ran while one was open for 1% of the time, Pallas kernels for 8%

profile of v2, /device:TPU:1, one launch (start us, length us, event | category | flops | bytes accessed | tf_op | source)
XLA Modules:
  0.0 71.5 jit_solution(15963287578366321012)
XLA Ops:
  0.6 0.0 copy-start
  0.6 4.3 %fourier.1 = (bf16[256,2,384]{2,1,0:T(2,128)(2,1)}, bf16[256,1440]{1,0:T(8,128)(2,1)}) custom-call(s32[1,128]{1,0:T(1,128)} %bitcast.10, bf16[2,288,1440]{2,1,0:T(8,128)(2,1)} %bitcast.8), custom_call_target="tpu_custom_call" | custom-call | tf_op jit(solution)/shard_map/fourier/pallas_call | solution.py:270
  5.0 15.7 %all-to-all-start = ((bf16[256,2,384]{2,1,0:T(2,128)(2,1)}), bf16[256,2,384]{2,1,0:T(2,128)(2,1)S(1)}, u32[]{:S(2)}, u32[]{:S(2)}) async-start(bf16[256,2,384]{2,1,0:T(2,128)(2,1)} %get-tuple-element.9), calls=%async_computation | async-start | bytes 786432 | tf_op jit(solution)/shard_map/all_to_all | solution.py:251
  20.7 0.0 copy-done
  20.7 0.6 dynamic_slice.3.z_ref
  21.3 0.1 pad_add_fusion.where_ref
  21.3 6.1 %basis.1 = (bf16[512,721]{1,0:T(8,128)(2,1)}, bf16[721,512]{1,0:T(8,128)(2,1)}, f32[40,768]{1,0:T(8,128)}) custom-call(s32[2]{0:T(128)S(1)} %pad_add_fusion.where_ref, bf16[721,2,512]{2,1,0:T(2,128)(2,1)} %bitcast.9, f32[36,2,2,721]{3,2,1,0:T(2,128)} %v_ref.1), custom_call_target="tpu_custom_call" | custom-call | flops 378011648 | bytes 4000000 | tf_op jit(solution)/shard_map/basis/pallas_call | solution.py:286
  27.4 11.9 %all-to-all-done.recv_ref = bf16[256,2,384]{2,1,0:T(2,128)(2,1)S(1)} async-done(((bf16[256,2,384]{2,1,0:T(2,128)(2,1)}), bf16[256,2,384]{2,1,0:T(2,128)(2,1)S(1)}, u32[]{:S(2)}, u32[]{:S(2)}) %all-to-all-start) | async-done | bytes 393248 | tf_op jit(solution)/shard_map/all_to_all | solution.py:251
  39.3 4.7 %crps.1 = bf16[256,2,384]{2,1,0:T(2,128)(2,1)S(1)} custom-call(s32[1]{0:T(128)} %dynamic_slice.3.z_ref, bf16[256,2,384]{2,1,0:T(2,128)(2,1)S(1)} %all-to-all-done.recv_ref, f32[40,768]{1,0:T(8,128)} %get-tuple-element.10.obs_far, bf16[512,721]{1,0:T(8,128)(2,1)} %get-tuple-element.11.pk_far, bf16[721,512]{1,0:T(8,128)(2,1)} %get-tuple-element.12.pl_far), custom_call_target="tpu_custom_call" | custom-call | tf_op jit(solution)/shard_map/crps/pallas_call | solution.py:310
  44.0 23.9 %all_to_all.10.recv_ref = bf16[256,2,384]{2,1,0:T(2,128)(2,1)S(1)} all-to-all(bf16[256,2,384]{2,1,0:T(2,128)(2,1)S(1)} %crps.1), channel_id=1, replica_groups=mesh['lat'=64,'ens'=4] {'ens','lat'}, dimensions={0} | all-to-all | bytes 786432 | tf_op jit(solution)/shard_map/all_to_all | solution.py:251
  67.9 3.6 %grid.1 = (bf16[2,288,1440]{2,1,0:T(8,128)(2,1)}, f32[2,2,36]{2,1,0:T(2,128)}) custom-call(s32[1]{0:T(128)} %bitcast.at_ref, bf16[256,2,384]{2,1,0:T(2,128)(2,1)S(1)} %all_to_all.10.recv_ref, bf16[256,1440]{1,0:T(8,128)(2,1)} %get-tuple-element.13.table_far), custom_call_target="tpu_custom_call" | custom-call | tf_op jit(solution)/shard_map/grid/pallas_call | solution.py:331
Async XLA Ops:
  0.6 20.0 %copy-start = (s32[128]{0:T(128)S(1)}, s32[128]{0:T(128)}, u32[]{:S(2)}) copy-start(s32[128]{0:T(128)} %param.7) | copy-start | bytes 1540
  5.0 34.3 %all-to-all-start = ((bf16[256,2,384]{2,1,0:T(2,128)(2,1)}), bf16[256,2,384]{2,1,0:T(2,128)(2,1)S(1)}, u32[]{:S(2)}, u32[]{:S(2)}) async-start(bf16[256,2,384]{2,1,0:T(2,128)(2,1)} %get-tuple-element.9), calls=%async_computation | async-start | bytes 786432 | tf_op jit(solution)/shard_map/all_to_all | solution.py:251

commit v3 on v2

--- a/solution.py
+++ b/solution.py
@@ -43,19 +43,35 @@
     wanted = 2 * lax.rem(d, lat) + lax.div(d, 2 * lat)
     waves.wait()
     z = jnp.sum(jnp.where(s == wanted, z_ref[...].astype(F32), 0.0), axis=1, keepdims=True)
-    dcol = lax.broadcasted_iota(jnp.int32, (count, 1), 0)
-    shift = (lax.rem(lax.div(dcol, lat), 2) * (nodes // 4)).astype(F32)
-    j = lax.broadcasted_iota(jnp.int32, (1, nodes), 1).astype(F32)
     step = 2.0 * math.pi / nodes
-    for a in range(0, count, 32):
-        p = j * z[a : a + 32] + shift[a : a + 32]
+
+    def cosine(p):
         p = p - nodes * jnp.floor(p * (1.0 / nodes))
         w = (jnp.abs(p - nodes / 2) - nodes / 4) * step
         w2 = w * w
         poly = -2.5052108e-08
         for c in (2.7557319e-06, -1.9841270e-04, 8.3333333e-03, -1.6666667e-01):
             poly = poly * w2 + c
-        table_ref[a : a + 32, :] = (w + w * (w2 * poly)).astype(BF16)
+        return w + w * (w2 * poly)
+
+    j = lax.broadcasted_iota(jnp.int32, (1, LANES), 1).astype(F32)
+    turn = nodes // 4
+    for half in range(count // (2 * lat)):
+        for a in range(0, lat, 16):
+            at = 2 * lat * half + a
+            wave = jnp.broadcast_to(z[at : at + 16], (16, LANES))
+            phase = wave * j
+            real, imag = cosine(phase), cosine(phase + turn)
+            ahead = wave * LANES
+            keep_part, swap_part = cosine(ahead), cosine(ahead + turn)
+            for b in range(0, nodes, LANES):
+                n = min(LANES, nodes - b)
+                table_ref[at : at + 16, b : b + n] = real[:, :n].astype(BF16)
+                table_ref[at + lat : at + lat + 16, b : b + n] = imag[:, :n].astype(BF16)
+                real, imag = (
+                    real * keep_part - imag * swap_part,
+                    imag * keep_part + real * swap_part,
+                )
     scale = nodes**-0.5
     keep = pltpu.make_async_copy(table_ref, table_far, sems.at[local])
     keep.start()
@@ -66,7 +82,7 @@
     keep.wait()
 
 
-def basis_kernel(lat, where_ref, p_ref, v_ref, pk_ref, pl_ref, obs_ref, p_vmem, v_vmem, mine, sems):
+def basis_kernel(lat, where_ref, p_ref, v_ref, basis_ref, obs_ref, p_vmem, v_vmem, mine, sems):
     slot = where_ref[0]
     first = pltpu.make_async_copy(p_ref, p_vmem, sems.at[0])
     second = pltpu.make_async_copy(v_ref.at[:, where_ref[1]], v_vmem, sems.at[1])
@@ -94,8 +110,7 @@
     target = lax.broadcasted_iota(jnp.int32, (lines, lines), 1)
     order = source == rows * lax.rem(target, lat) + lax.div(target, lat)
     turned = dot(mine[...], order.astype(F32).astype(BF16), ((1,), (0,)))
-    pl_ref[...] = turned.astype(BF16)
-    pk_ref[...] = turned.T.astype(BF16)
+    basis_ref[...] = turned.astype(BF16)
     second.wait()
     seen = v_vmem[...]
     obs_ref[...] = jnp.zeros(obs_ref.shape, F32)
@@ -104,15 +119,9 @@
 
 def crps_kernel(
     lat, ens, degrees, variables,
-    z_ref, recv_ref, obs_far, pk_far, pl_far, send_ref,
-    turned, spectra, coeffs, grads, back, obs_ref, pk_ref, pl_ref, sems,
+    z_ref, recv_ref, obs_ref, basis_ref, send_ref,
+    turned, spectra, coeffs, grads, back,
 ):
-    copies = [
-        pltpu.make_async_copy(far, near, sems.at[c])
-        for c, (far, near) in enumerate(((pk_far, pk_ref), (obs_far, obs_ref), (pl_far, pl_ref)))
-    ]
-    for copy in copies:
-        copy.start()
     local = MEMBERS // ens
     pairs = ens // 2
     for m in range(local):
@@ -130,10 +139,8 @@
                 spectra[pl.ds(e * VROWS, VROWS), into] = jnp.where(low, even, pltpu.roll(odd, lat, 1))
                 e = e + local
                 spectra[pl.ds(e * VROWS, VROWS), into] = jnp.where(low, pltpu.roll(even, lat, 1), odd)
-    copies[0].wait()
-    coeffs[:, :degrees] = dot(spectra[...].astype(BF16), pk_ref[...], ((1,), (0,)))
-
-    copies[1].wait()
+    coeffs[:, :degrees] = dot(spectra[...].astype(BF16), basis_ref[...], ((1,), (1,)))
+
     zonal = z_ref[0]
     factor = jnp.where(zonal == 0, 1.0, 2.0).astype(F32)
     tiles = VROWS // 8
@@ -180,8 +187,7 @@
     zero = jnp.zeros((8, LANES), F32)
     totals = lax.fori_loop(0, blocks, one_block, (zero,) * tiles)
 
-    copies[2].wait()
-    returned = dot(grads[:, :degrees], pl_ref[...], ((1,), (0,)))
+    returned = dot(grads[:, :degrees], basis_ref[...], ((1,), (0,)))
     for m in range(local):
         for t2 in range(4):
             for k2 in range(pairs):
@@ -207,16 +213,12 @@
             send_ref[k2 * LANES : (k2 + 1) * LANES, m, :] = back[m, k2].T.astype(BF16)
 
 
-def grid_kernel(lat, ens, variables, at_ref, recv_ref, table_far, out_ref, score_ref, block, table_ref, sems):
-    load = pltpu.make_async_copy(table_far, table_ref, sems.at[6])
-    load.start()
+def grid_kernel(lat, ens, variables, at_ref, recv_ref, table_ref, out_ref, score_ref, block, sems):
     local, span, nodes = out_ref.shape
     scale = nodes**-0.5
     copies = []
     for m in range(local):
         turned = recv_ref[:, m, :].astype(F32).T.astype(BF16)
-        if m == 0:
-            load.wait()
         for a in range(0, span, LANES):
             n = min(LANES, span - a)
             part = dot(turned[a : a + n, :], table_ref[...], ((1,), (0,))) * scale
@@ -283,16 +285,15 @@
     )(*far_of(zonal_order_values.reshape(1, -1), predicted_grid.reshape(local, span, nodes)))
     recv = exchange(send)
 
-    by_line, by_degree, observed = pl.pallas_call(
+    basis, observed = pl.pallas_call(
         functools.partial(basis_kernel, lat),
         name="basis",
         compiler_params=PARAMS,
         in_specs=[scalar, far, far],
-        out_specs=[whole, whole, whole],
+        out_specs=[whole, whole],
         out_shape=[
-            pltpu.HBM((all_lines, degrees), BF16),
-            pltpu.HBM((degrees, all_lines), BF16),
-            pltpu.HBM((VROWS, padded), F32),
+            jax.ShapeDtypeStruct((degrees, all_lines), BF16),
+            jax.ShapeDtypeStruct((VROWS, padded), F32),
         ],
         scratch_shapes=[
             VMEM((degrees, slots, all_lines), BF16),
@@ -311,7 +312,7 @@
         functools.partial(crps_kernel, lat, ens, degrees, variables),
         name="crps",
         compiler_params=PARAMS,
-        in_specs=[scalar, whole, far, far, far],
+        in_specs=[scalar, whole, whole, whole],
         out_specs=whole,
         out_shape=sent,
         scratch_shapes=[
@@ -320,19 +321,15 @@
             VMEM((MEMBERS * VROWS, padded), F32),
             VMEM((MEMBERS * VROWS, padded), BF16),
             VMEM((local, ens // 2, WIDTH, LANES), F32),
-            VMEM((VROWS, padded), F32),
-            VMEM((all_lines, degrees), BF16),
-            VMEM((degrees, all_lines), BF16),
-            pltpu.SemaphoreType.DMA((3,)),
-        ],
-    )(own_wave, recv, *far_of(observed, by_line, by_degree))
+        ],
+    )(own_wave, recv, observed, basis)
     recv = exchange(send)
 
     sensitivity, scores = pl.pallas_call(
         functools.partial(grid_kernel, lat, ens, variables),
         name="grid",
         compiler_params=PARAMS,
-        in_specs=[scalar, whole, far],
+        in_specs=[scalar, whole, whole],
         out_specs=[far, whole],
         out_shape=[
             jax.ShapeDtypeStruct((local, span, nodes), BF16),
@@ -340,10 +337,9 @@
         ],
         scratch_shapes=[
             VMEM((local, span, nodes), BF16),
-            VMEM((count, nodes), BF16),
-            pltpu.SemaphoreType.DMA((7,)),
-        ],
-    )(at_lat.reshape(1), recv, *far_of(table))
+            pltpu.SemaphoreType.DMA((6,)),
+        ],
+    )(at_lat.reshape(1), recv, table)
     return sensitivity.reshape(predicted_grid.shape), scores.transpose(2, 0, 1)
 
 

time: 71.8 us -> 69.1 us (0.962)
  Pallas kernels: 18.7 us -> 15 us
  waiting for transfers between devices: 11.9 us -> 12.9 us
    pallas_call x1, Pallas kernels: 6.06 us -> 4.92 us  [body(): pl.pallas_call(functools.partial(basis_kernel, lat), name='basis', compil...]
    all_to_all x1, waiting for transfers between devices: 11.9 us -> 12.9 us  [exchange(): return lax.all_to_all(values, MESH_AXES, 0, 0, tiled=True)]
    pallas_call x1, Pallas kernels: 3.63 us -> 2.61 us  [body(): pl.pallas_call(functools.partial(grid_kernel, lat, ens, variables), name=...]
    pallas_call x1, Pallas kernels: 4.33 us -> 3.33 us  [body(): pl.pallas_call(functools.partial(fourier_kernel, lat), name='fourier', co...]
  transfers between devices with their start and end apart: 1 -> 1, of which waited for: 1 -> 1; matrix products, arithmetic and copies ran while one was open for 1% -> 1% of each run, Pallas kernels for 8% -> 7%
where the time goes in v3:
time: 69.1 us; the launch traced here: 68.9 us
  blocking collectives  23.9 us (35%)
  starting transfers between devices  15.6 us (23%)
  Pallas kernels  15 us (22%)
  waiting for transfers between devices  12.9 us (19%)
  between operations  0.7 us (1%)
    all_to_all x1, blocking collectives, exchange(): return lax.all_to_all(values, MESH_AXES, 0, 0, tiled=True)  23.9 us
    all_to_all x1, starting transfers between devices, exchange(): return lax.all_to_all(values, MESH_AXES, 0, 0, tiled=True)  15.6 us
    all_to_all x1, waiting for transfers between devices, exchange(): return lax.all_to_all(values, MESH_AXES, 0, 0, tiled=True)  12.9 us
    pallas_call x1, Pallas kernels, body(): pl.pallas_call(functools.partial(basis_kernel, lat), name='basis', compil...  4.92 us
    pallas_call x1, Pallas kernels, body(): pl.pallas_call(functools.partial(crps_kernel, lat, ens, degrees, variable...  4.09 us
    pallas_call x1, Pallas kernels, body(): pl.pallas_call(functools.partial(fourier_kernel, lat), name='fourier', co...  3.33 us
    pallas_call x1, Pallas kernels, body(): pl.pallas_call(functools.partial(grid_kernel, lat, ens, variables), name=...  2.61 us
  transfers between devices with their start and end apart: 1, of which 1 were waited for; matrix products, arithmetic and copies ran while one was open for 1% of the time, Pallas kernels for 7%

profile of v3, /device:TPU:1, one launch (start us, length us, event | category | flops | bytes accessed | tf_op | source)
XLA Modules:
  0.0 68.9 jit_solution(9790747229230384140)
XLA Ops:
  0.6 0.0 copy-start.1
  0.6 3.3 %fourier.1 = (bf16[256,2,384]{2,1,0:T(2,128)(2,1)}, bf16[256,1440]{1,0:T(8,128)(2,1)}) custom-call(s32[1,128]{1,0:T(1,128)} %bitcast.10, bf16[2,288,1440]{2,1,0:T(8,128)(2,1)} %bitcast.8), custom_call_target="tpu_custom_call" | custom-call | tf_op jit(solution)/shard_map/fourier/pallas_call | solution.py:272
  4.0 15.6 %all-to-all-start = ((bf16[256,2,384]{2,1,0:T(2,128)(2,1)}), bf16[256,2,384]{2,1,0:T(2,128)(2,1)S(1)}, u32[]{:S(2)}, u32[]{:S(2)}) async-start(bf16[256,2,384]{2,1,0:T(2,128)(2,1)} %get-tuple-element.8), calls=%async_computation | async-start | bytes 786432 | tf_op jit(solution)/shard_map/all_to_all | solution.py:253
  19.7 0.0 copy-done.1
  19.7 0.7 dynamic_slice.3.z_ref
  20.3 0.1 pad_add_fusion.where_ref
  20.4 0.0 copy-start
  20.4 4.9 %basis.1 = (bf16[721,512]{1,0:T(8,128)(2,1)S(1)}, f32[40,768]{1,0:T(8,128)S(1)}) custom-call(s32[2]{0:T(128)S(1)} %pad_add_fusion.where_ref, bf16[721,2,512]{2,1,0:T(2,128)(2,1)} %bitcast.9, f32[36,2,2,721]{3,2,1,0:T(2,128)} %v_ref.1), custom_call_target="tpu_custom_call" | custom-call | flops 378011648 | bytes 4000000 | tf_op jit(solution)/shard_map/basis/pallas_call | solution.py:288
  25.3 12.9 %all-to-all-done.recv_ref = bf16[256,2,384]{2,1,0:T(2,128)(2,1)S(1)} async-done(((bf16[256,2,384]{2,1,0:T(2,128)(2,1)}), bf16[256,2,384]{2,1,0:T(2,128)(2,1)S(1)}, u32[]{:S(2)}, u32[]{:S(2)}) %all-to-all-start) | async-done | bytes 393248 | tf_op jit(solution)/shard_map/all_to_all | solution.py:253
  38.3 4.1 %crps.1 = bf16[256,2,384]{2,1,0:T(2,128)(2,1)S(1)} custom-call(s32[1]{0:T(128)} %dynamic_slice.3.z_ref, bf16[256,2,384]{2,1,0:T(2,128)(2,1)S(1)} %all-to-all-done.recv_ref, f32[40,768]{1,0:T(8,128)S(1)} %get-tuple-element.9.obs_ref, bf16[721,512]{1,0:T(8,128)(2,1)S(1)} %get-tuple-element.10.basis_ref), custom_call_target="tpu_custom_call" | custom-call | tf_op jit(solution)/shard_map/crps/pallas_call | solution.py:311
  42.4 23.9 %all_to_all.10.recv_ref = bf16[256,2,384]{2,1,0:T(2,128)(2,1)S(1)} all-to-all(bf16[256,2,384]{2,1,0:T(2,128)(2,1)S(1)} %crps.1), channel_id=1, replica_groups=mesh['lat'=64,'ens'=4] {'ens','lat'}, dimensions={0} | all-to-all | bytes 786432 | tf_op jit(solution)/shard_map/all_to_all | solution.py:253
  66.3 0.0 copy-done
  66.3 2.6 %grid.1 = (bf16[2,288,1440]{2,1,0:T(8,128)(2,1)}, f32[2,2,36]{2,1,0:T(2,128)}) custom-call(s32[1]{0:T(128)} %bitcast.at_ref, bf16[256,2,384]{2,1,0:T(2,128)(2,1)S(1)} %all_to_all.10.recv_ref, bf16[256,1440]{1,0:T(8,128)(2,1)S(1)} %copy-done), custom_call_target="tpu_custom_call" | custom-call | tf_op jit(solution)/shard_map/grid/pallas_call | solution.py:328
Async XLA Ops:
  0.6 19.0 %copy-start.1 = (s32[128]{0:T(128)S(1)}, s32[128]{0:T(128)}, u32[]{:S(2)}) copy-start(s32[128]{0:T(128)} %param.7) | copy-start | bytes 1540
  4.0 34.3 %all-to-all-start = ((bf16[256,2,384]{2,1,0:T(2,128)(2,1)}), bf16[256,2,384]{2,1,0:T(2,128)(2,1)S(1)}, u32[]{:S(2)}, u32[]{:S(2)}) async-start(bf16[256,2,384]{2,1,0:T(2,128)(2,1)} %get-tuple-element.8), calls=%async_computation | async-start | bytes 786432 | tf_op jit(solution)/shard_map/all_to_all | solution.py:253
  20.4 45.9 %copy-start = (bf16[256,1440]{1,0:T(8,128)(2,1)S(1)}, bf16[256,1440]{1,0:T(8,128)(2,1)}, u32[]{:S(2)}) copy-start(bf16[256,1440]{1,0:T(8,128)(2,1)} %get-tuple-element.11.table_ref) | copy-start | bytes 2211844

commit v4 on v3

v4 whole, which is shorter than its diff:
```python
import functools
import math

import jax
import jax.numpy as jnp
from jax import lax
from jax.experimental import pallas as pl
from jax.experimental.pallas import tpu as pltpu
from jax.sharding import Mesh, PartitionSpec as P

SMOOTH = 0.1
LANES = 128
VROWS = 40
WIDTH = 640
MEMBERS = 8
F32 = jnp.float32
BF16 = jnp.bfloat16
VMEM = pltpu.VMEM
PARAMS = pltpu.CompilerParams(vmem_limit_bytes=16 * 1024 * 1024)
GROUP = ("ens", "chip")


def dot(a, b, dims):
    return lax.dot_general(a, b, (dims, ((), ())), preferred_element_type=F32)


def fourier_kernel(chips, core_ref, z_far, x_ref, send_ref, table_far, z_ref, x_vmem, table_ref, sems):
    width, nodes = x_vmem.shape
    rows = x_ref.shape[0]
    waves = pltpu.make_async_copy(z_far, z_ref, sems.at[0])
    waves.start()
    half = rows // 2
    copies = [
        pltpu.make_async_copy(x_ref.at[pl.ds(a, half)], x_vmem.at[pl.ds(a, half)], sems.at[1 + a // half])
        for a in range(0, rows, half)
    ]
    for copy in copies:
        copy.start()
    x_vmem[rows:, :] = jnp.zeros((width - rows, nodes), BF16)
    count = table_ref.shape[0]
    group = count // 2
    core = core_ref[0]
    shape = (count, z_ref.shape[1])
    d = lax.broadcasted_iota(jnp.int32, shape, 0)
    s = lax.broadcasted_iota(jnp.int32, shape, 1)
    other = lax.div(d, group)
    their_core = core + other - 2 * core * other
    slot = lax.div(lax.rem(d, group), 2 * chips)
    wanted = 2 * (2 * lax.rem(d, chips) + their_core) + slot
    waves.wait()
    z = jnp.sum(jnp.where(s == wanted, z_ref[...].astype(F32), 0.0), axis=1, keepdims=True)
    step = 2.0 * math.pi / nodes

    def cosine(p):
        p = p - nodes * jnp.floor(p * (1.0 / nodes))
        w = (jnp.abs(p - nodes / 2) - nodes / 4) * step
        w2 = w * w
        poly = -2.5052108e-08
        for c in (2.7557319e-06, -1.9841270e-04, 8.3333333e-03, -1.6666667e-01):
            poly = poly * w2 + c
        return w + w * (w2 * poly)

    j = lax.broadcasted_iota(jnp.int32, (1, LANES), 1).astype(F32)
    turn = nodes // 4
    for base in range(0, count, 2 * chips):
        for at in range(base, base + chips, 16):
            wave = jnp.broadcast_to(z[at : at + 16], (16, LANES))
            phase = wave * j
            real, imag = cosine(phase), cosine(phase + turn)
            ahead = wave * LANES
            keep_part, swap_part = cosine(ahead), cosine(ahead + turn)
            for b in range(0, nodes, LANES):
                n = min(LANES, nodes - b)
                table_ref[at : at + 16, b : b + n] = real[:, :n].astype(BF16)
                table_ref[at + chips : at + chips + 16, b : b + n] = imag[:, :n].astype(BF16)
                real, imag = (
                    real * keep_part - imag * swap_part,
                    imag * keep_part + real * swap_part,
                )
    keep = pltpu.make_async_copy(table_ref, table_far, sems.at[3])
    keep.start()
    for copy in copies:
        copy.wait()
    spectra = dot(table_ref[...], x_vmem[...], ((1,), (1,))) * nodes**-0.5
    for q in range(2):
        send_ref[:, q, :] = spectra[q * group : (q + 1) * group].astype(BF16)
    keep.wait()


def basis_kernel(chips, where_ref, p_ref, v_ref, basis_ref, obs_ref, p_vmem, v_vmem, mine, sems):
    slot = where_ref[0]
    core = where_ref[2]
    first = pltpu.make_async_copy(p_ref, p_vmem, sems.at[0])
    second = pltpu.make_async_copy(v_ref.at[:, where_ref[1]], v_vmem, sems.at[1])
    first.start()
    second.start()
    degrees, _, lines = p_vmem.shape
    first.wait()
    step = 16

    def pick(start, size):
        both = p_vmem[pl.ds(start, size)].astype(F32)
        chosen = jnp.where(slot == 0, both[:, 0, :], both[:, 1, :])
        mine[pl.ds(start, size), :] = chosen.astype(BF16)

    def one(i, carry):
        pick(pl.multiple_of(i * step, step), step)
        return carry

    lax.fori_loop(0, degrees // step, one, 0)
    rest = degrees % step
    if rest:
        pick(degrees - rest, rest)
    rows = lines // (2 * chips)
    source = lax.broadcasted_iota(jnp.int32, (lines, lines), 0)
    target = lax.broadcasted_iota(jnp.int32, (lines, lines), 1)
    other = lax.rem(lax.div(target, chips), 2)
    their_core = core + other - 2 * core * other
    line = rows * (2 * lax.rem(target, chips) + their_core) + lax.div(target, 2 * chips)
    order = source == line
    turned = dot(mine[...], order.astype(F32).astype(BF16), ((1,), (0,)))
    basis_ref[...] = turned.astype(BF16)
    second.wait()
    seen = v_vmem[...]
    obs_ref[...] = jnp.zeros(obs_ref.shape, F32)
    obs_ref[: seen.shape[0], :degrees] = jnp.where(slot == 0, seen[:, 0, :], seen[:, 1, :])


def swap_groups(parts, chips):
    lane = lax.broadcasted_iota(jnp.int32, parts[0].shape, 1)
    for distance in (2, 1):
        low = lax.rem(lax.div(lane, chips * distance), 2) == 0
        shift = chips * distance
        out = [None] * 4
        for j in range(4):
            if j & distance:
                continue
            a, b = parts[j], parts[j + distance]
            out[j] = jnp.where(low, a, pltpu.roll(b, shift, 1))
            out[j + distance] = jnp.where(low, pltpu.roll(a, LANES - shift, 1), b)
        parts = out
    return parts


def crps_kernel(
    chips, ens, degrees, variables,
    z_ref, own_ref, partner_ref, obs_ref, basis_ref, send_ref,
    turned, spectra, coeffs, grads, back,
):
    local = MEMBERS // ens
    span = variables * 8
    for q, ref in enumerate((own_ref, partner_ref)):
        turned[q] = ref[:, q, :].astype(F32).T
    for t2 in range(4):
        for m in range(local):
            parts = [
                turned[j % 2, pl.ds(m * span + 2 * t2 + j // 2, VROWS, stride=8), :] for j in range(4)
            ]
            for k, part in enumerate(swap_groups(parts, chips)):
                e = k * local + m
                spectra[pl.ds(e * VROWS, VROWS), pl.ds(t2 * LANES, LANES)] = part
    coeffs[:, :degrees] = dot(spectra[...].astype(BF16), basis_ref[...], ((1,), (1,)))

    zonal = z_ref[0]
    factor = jnp.where(zonal == 0, 1.0, 2.0).astype(F32)
    tiles = VROWS // 8

    def one_block(b, totals):
        lanes = pl.ds(pl.multiple_of(b * LANES, LANES), LANES)
        degree = b * LANES + lax.broadcasted_iota(jnp.int32, (8, LANES), 1)
        active = (degree >= zonal) & (degree < degrees)
        sums = []
        for tile in range(tiles):
            c = [coeffs[pl.ds(e * VROWS + tile * 8, 8), lanes] for e in range(MEMBERS)]
            seen = obs_ref[pl.ds(tile * 8, 8), lanes]
            slope = [None] * MEMBERS
            spread = None
            for e in range(MEMBERS - 1):
                part = None
                for f in range(e + 1, MEMBERS):
                    gap = c[e] - c[f]
                    square = gap * gap + SMOOTH * SMOOTH
                    inverse = lax.rsqrt(square)
                    sign = gap * inverse
                    root = square * inverse
                    part = root if part is None else part + root
                    slope[e] = sign if slope[e] is None else slope[e] + sign
                    slope[f] = -sign if slope[f] is None else slope[f] - sign
                part = part - SMOOTH * (MEMBERS - 1 - e)
                spread = part if spread is None else spread + part
            miss = None
            for e in range(MEMBERS):
                gap = c[e] - seen
                square = gap * gap + SMOOTH * SMOOTH
                inverse = lax.rsqrt(square)
                root = square * inverse
                miss = root if miss is None else miss + root
                grad = factor * (gap * inverse * (1 / MEMBERS) - slope[e] * (1 / MEMBERS**2))
                grad = jnp.where(active, grad, 0.0)
                grads[pl.ds(e * VROWS + tile * 8, 8), lanes] = grad.astype(BF16)
            miss = miss - SMOOTH * MEMBERS
            score = miss * (1 / MEMBERS) - spread * (1 / MEMBERS**2)
            sums.append(totals[tile] + jnp.where(active, factor * score, 0.0))
        return tuple(sums)

    blocks = coeffs.shape[1] // LANES
    zero = jnp.zeros((8, LANES), F32)
    totals = lax.fori_loop(0, blocks, one_block, (zero,) * tiles)

    returned = dot(grads[:, :degrees], basis_ref[...], ((1,), (0,)))
    for m in range(local):
        for t2 in range(4):
            parts = []
            for k in range(ens):
                e = k * local + m
                parts.append(returned[e * VROWS : (e + 1) * VROWS, t2 * LANES : (t2 + 1) * LANES])
            for j, part in enumerate(swap_groups(parts, chips)):
                back[j % 2, pl.ds(m * span + 2 * t2 + j // 2, VROWS, stride=8), :] = part
    base = local * span
    for tile in range(tiles):
        rest = jnp.sum(totals[tile], axis=1, keepdims=True) * (1.0 / degrees)
        for q in range(2):
            piece = rest.astype(BF16).astype(F32)
            rest = rest - piece
            back[q, pl.ds(base + tile * 8, 8), :] = jnp.broadcast_to(piece, (8, LANES))
    for q in range(2):
        back[q, base + VROWS :, :] = jnp.zeros((WIDTH - base - VROWS, LANES), F32)
        send_ref[:, q, :] = back[q].T.astype(BF16)


def grid_kernel(chips, ens, variables, at_ref, own_ref, partner_ref, table_ref, out_ref, score_ref, block, sems):
    rows, nodes = out_ref.shape
    scale = nodes**-0.5
    turned = jnp.concatenate(
        [ref[:, q, :].astype(F32).T.astype(BF16) for q, ref in enumerate((own_ref, partner_ref))], axis=1
    )
    copies = []
    for a in range(0, rows, LANES):
        n = min(LANES, rows - a)
        part = dot(turned[a : a + n, :], table_ref[...], ((1,), (0,))) * scale
        block[a : a + n, :] = part.astype(BF16)
        copy = pltpu.make_async_copy(block.at[pl.ds(a, n)], out_ref.at[pl.ds(a, n)], sems.at[len(copies)])
        copy.start()
        copies.append(copy)
    base = WIDTH - LANES
    mine = lax.broadcasted_iota(jnp.int32, (chips, LANES), 0) == at_ref[0]
    for k in range(ens):
        total = None
        for q in range(2):
            term = own_ref[k * chips : (k + 1) * chips, q, base:].astype(F32)
            term = jnp.sum(jnp.where(mine, term, 0.0), axis=0, keepdims=True)
            total = term if total is None else total + term
        total = pltpu.roll(total, LANES - (rows - base), 1)
        score_ref[k % 2, k // 2 : k // 2 + 1, :] = total[:, :variables]
    for copy in copies:
        copy.wait()


def far_of(*arrays):
    return [pltpu.with_memory_space_constraint(a, pltpu.HBM) for a in arrays]


def to_chips(values):
    return lax.all_to_all(values, GROUP, 0, 0, tiled=True)


def from_partner(values):
    return lax.ppermute(values, "core", [(0, 1), (1, 0)])


def body(predicted_grid, verifying_coefficients, weighted_polynomial_values, zonal_order_values):
    local, variables, lines, nodes = predicted_grid.shape
    slots, all_lines, degrees = weighted_polynomial_values.shape
    chips = lax.axis_size("chip")
    ens = lax.axis_size("ens")
    group = chips * ens
    count = 2 * group
    rows = local * variables * lines
    padded = -(-degrees // LANES) * LANES
    whole = pl.BlockSpec(memory_space=VMEM)
    scalar = pl.BlockSpec(memory_space=pltpu.SMEM)
    far = pl.BlockSpec(memory_space=pltpu.HBM)
    chip = lax.axis_index("chip")
    core = lax.axis_index("core")
    at_ens = lax.axis_index("ens")
    slot = at_ens // 2
    sent = jax.ShapeDtypeStruct((group, 2, WIDTH), BF16)

    send, table = pl.pallas_call(
        functools.partial(fourier_kernel, chips),
        name="fourier",
        compiler_params=PARAMS,
        in_specs=[scalar, far, far],
        out_specs=[whole, far],
        out_shape=[sent, pltpu.HBM((count, nodes), BF16)],
        scratch_shapes=[
            VMEM((1, zonal_order_values.shape[0]), jnp.int32),
            VMEM((WIDTH, nodes), BF16),
            VMEM((count, nodes), BF16),
            pltpu.SemaphoreType.DMA((4,)),
        ],
    )(core.reshape(1), *far_of(zonal_order_values.reshape(1, -1), predicted_grid.reshape(rows, nodes)))
    own = to_chips(send)

    basis, observed = pl.pallas_call(
        functools.partial(basis_kernel, chips),
        name="basis",
        compiler_params=PARAMS,
        in_specs=[scalar, far, far],
        out_specs=[whole, whole],
        out_shape=[
            jax.ShapeDtypeStruct((degrees, all_lines), BF16),
            jax.ShapeDtypeStruct((VROWS, padded), F32),
        ],
        scratch_shapes=[
            VMEM((degrees, slots, all_lines), BF16),
            VMEM((variables, slots, degrees), F32),
            VMEM((degrees, all_lines), BF16),
            pltpu.SemaphoreType.DMA((2,)),
        ],
        cost_estimate=pl.CostEstimate(flops=2 * degrees * all_lines**2, bytes_accessed=4_000_000, transcendentals=0),
    )(
        jnp.stack([slot, at_ens % 2, core]),
        *far_of(weighted_polynomial_values.transpose(2, 0, 1), verifying_coefficients),
    )
    own, basis, observed = lax.optimization_barrier((own, basis, observed))
    partner = from_partner(own)
    own_wave = lax.dynamic_slice_in_dim(zonal_order_values, 2 * (2 * chip + core) + slot, 1)

    send = pl.pallas_call(
        functools.partial(crps_kernel, chips, ens, degrees, variables),
        name="crps",
        compiler_params=PARAMS,
        in_specs=[scalar, whole, whole, whole, whole],
        out_specs=whole,
        out_shape=sent,
        scratch_shapes=[
            VMEM((2, WIDTH, LANES), F32),
            VMEM((MEMBERS * VROWS, all_lines), F32),
            VMEM((MEMBERS * VROWS, padded), F32),
            VMEM((MEMBERS * VROWS, padded), BF16),
            VMEM((2, WIDTH, LANES), F32),
        ],
    )(own_wave, own, partner, observed, basis)
    own = to_chips(send)
    partner = from_partner(own)

    sensitivity, scores = pl.pallas_call(
        functools.partial(grid_kernel, chips, ens, variables),
        name="grid",
        compiler_params=PARAMS,
        in_specs=[scalar, whole, whole, whole],
        out_specs=[far, whole],
        out_shape=[
            jax.ShapeDtypeStruct((rows, nodes), BF16),
            jax.ShapeDtypeStruct((2, 2, variables), F32),
        ],
        scratch_shapes=[VMEM((rows, nodes), BF16), pltpu.SemaphoreType.DMA((5,))],
    )(chip.reshape(1), own, partner, table)
    return sensitivity.reshape(predicted_grid.shape), scores.transpose(2, 0, 1)


def solution(mesh):
    lat, ens = mesh.devices.shape
    fine = Mesh(mesh.devices.reshape(lat // 2, 2, ens), ("chip", "core", "ens"))
    block = ("chip", "core")
    placed = (P("ens", None, block, None), P(None, None, block, None), P(block, None, None), P())
    return jax.shard_map(
        body,
        mesh=fine,
        in_specs=placed,
        out_specs=(P("ens", None, block, None), P(None, None, block)),
        check_vma=False,
    )
```

time: 69.1 us -> 67.5 us (0.977)
  starting transfers between devices: 15.6 us -> 23.2 us
  blocking collectives: 23.9 us -> 19 us
  waiting for transfers between devices: 12.9 us -> 9.13 us
    ppermute x0 -> x2, starting transfers between devices: none -> 6.81 us  [from_partner(): return lax.ppermute(values, 'core', [(0, 1), (1, 0)])]
    all_to_all x1, waiting for transfers between devices: 12.9 us -> 7.2 us  [to_chips(): return lax.all_to_all(values, GROUP, 0, 0, tiled=True)]
    all_to_all x1, blocking collectives: 23.9 us -> 19 us  [to_chips(): return lax.all_to_all(values, GROUP, 0, 0, tiled=True)]
    ppermute x0 -> x2, waiting for transfers between devices: none -> 1.93 us  [from_partner(): return lax.ppermute(values, 'core', [(0, 1), (1, 0)])]
    all_to_all x1, starting transfers between devices: 15.6 us -> 16.3 us  [to_chips(): return lax.all_to_all(values, GROUP, 0, 0, tiled=True)]
  transfers between devices with their start and end apart: 1 -> 3, of which waited for: 1 -> 3; matrix products, arithmetic and copies ran while one was open for 1% -> 1% of each run, Pallas kernels for 7% -> 7%
where the time goes in v4:
time: 67.5 us; the launch traced here: 67.2 us
  starting transfers between devices  23.2 us (34%)
  blocking collectives  19 us (28%)
  Pallas kernels  14.6 us (22%)
  waiting for transfers between devices  9.13 us (14%)
  between operations  0.7 us (1%)
    all_to_all x1, blocking collectives, to_chips(): return lax.all_to_all(values, GROUP, 0, 0, tiled=True)  19 us
    all_to_all x1, starting transfers between devices, to_chips(): return lax.all_to_all(values, GROUP, 0, 0, tiled=True)  16.3 us
    all_to_all x1, waiting for transfers between devices, to_chips(): return lax.all_to_all(values, GROUP, 0, 0, tiled=True)  7.2 us
    ppermute x2, starting transfers between devices, from_partner(): return lax.ppermute(values, 'core', [(0, 1), (1, 0)])  6.81 us
    pallas_call x1, Pallas kernels, body(): pl.pallas_call(functools.partial(basis_kernel, chips), name='basis', comp...  4.93 us
    pallas_call x1, Pallas kernels, body(): pl.pallas_call(functools.partial(crps_kernel, chips, ens, degrees, variab...  4.14 us
    pallas_call x1, Pallas kernels, body(): pl.pallas_call(functools.partial(fourier_kernel, chips), name='fourier',...  3.13 us
    pallas_call x1, Pallas kernels, body(): pl.pallas_call(functools.partial(grid_kernel, chips, ens, variables), nam...  2.43 us
  transfers between devices with their start and end apart: 3, of which 3 were waited for; matrix products, arithmetic and copies ran while one was open for 1% of the time, Pallas kernels for 7%

profile of v4, /device:TPU:1, one launch (start us, length us, event | category | flops | bytes accessed | tf_op | source)
XLA Modules:
  0.0 67.2 jit_solution(13404742857327137746)
XLA Ops:
  0.6 0.0 copy-start.1
  0.6 3.1 %fourier.1 = (bf16[128,2,640]{2,1,0:T(2,128)(2,1)}, bf16[256,1440]{1,0:T(8,128)(2,1)}) custom-call(s32[1]{0:T(128)} %bitcast.1.core_ref, s32[1,128]{1,0:T(1,128)} %bitcast.11, bf16[576,1440]{1,0:T(8,128)(2,1)} %bitcast.9), custom_call_target="tpu_custom_call" | custom-call | tf_op jit(solution)/shard_map/fourier/pallas_call | solution.py:289
  3.8 16.3 %all-to-all-start = ((bf16[128,2,640]{2,1,0:T(2,128)(2,1)}), bf16[128,2,640]{2,1,0:T(2,128)(2,1)S(1)}, u32[]{:S(2)}, u32[]{:S(2)}) async-start(bf16[128,2,640]{2,1,0:T(2,128)(2,1)} %get-tuple-element.11), calls=%async_computation | async-start | bytes 655360 | tf_op jit(solution)/shard_map/all_to_all | solution.py:264
  20.2 0.1 pad_add_fusion.where_ref
  20.2 0.0 copy-start
  20.2 4.9 %basis.1 = (bf16[721,512]{1,0:T(8,128)(2,1)S(1)}, f32[40,768]{1,0:T(8,128)S(1)}) custom-call(s32[3]{0:T(128)S(1)} %pad_add_fusion.where_ref, bf16[721,2,512]{2,1,0:T(2,128)(2,1)} %bitcast.10, f32[36,2,2,721]{3,2,1,0:T(2,128)} %v_ref.1), custom_call_target="tpu_custom_call" | custom-call | flops 378011648 | bytes 4000000 | tf_op jit(solution)/shard_map/basis/pallas_call | solution.py:305
  25.2 7.2 %all-to-all-done.own_ref = bf16[128,2,640]{2,1,0:T(2,128)(2,1)S(1)} async-done(((bf16[128,2,640]{2,1,0:T(2,128)(2,1)}), bf16[128,2,640]{2,1,0:T(2,128)(2,1)S(1)}, u32[]{:S(2)}, u32[]{:S(2)}) %all-to-all-start) | async-done | bytes 327712 | tf_op jit(solution)/shard_map/all_to_all | solution.py:264
  32.4 3.6 %collective-permute-start = (bf16[128,2,640]{2,1,0:T(2,128)(2,1)S(1)}, bf16[128,2,640]{2,1,0:T(2,128)(2,1)S(1)}, u32[]{:S(2)}, u32[]{:S(2)}) collective-permute-start(bf16[128,2,640]{2,1,0:T(2,128)(2,1)S(1)} %all-to-all-done.own_ref), channel_id=1, source_target_pairs={{0,4},{4,0},{1,5},{5,1},{2,6},{6,2},{3,7},{7,3},{8,12},{12,8},{9,1... | collective-permute-start | bytes 983048 | tf_op jit(solution)/shard_map/ppermute | solution.py:268
  35.9 0.0 copy-done.1
  35.9 0.6 dynamic_slice.3.z_ref
  36.5 0.7 collective-permute-done.partner_ref
  37.2 4.1 %crps.1 = bf16[128,2,640]{2,1,0:T(2,128)(2,1)S(1)} custom-call(s32[1]{0:T(128)} %dynamic_slice.3.z_ref, bf16[128,2,640]{2,1,0:T(2,128)(2,1)S(1)} %all-to-all-done.own_ref, bf16[128,2,640]{2,1,0:T(2,128)(2,1)S(1)} %collective-permute-done.partner_ref, f32[40,768]{1,0:T(8,128)S(1)} %get-tuple-element.15.obs_ref, bf16[721,512]{1,0:T(8,128)(2,1)S(1)} %get-tuple-element.16.basis_ref), custom_call_target="tpu_custom_call" | custom-call | tf_op jit(solution)/shard_map/crps/pallas_call | solution.py:330
  41.3 19.0 %all_to_all.10.own_ref = bf16[128,2,640]{2,1,0:T(2,128)(2,1)S(1)} all-to-all(bf16[128,2,640]{2,1,0:T(2,128)(2,1)S(1)} %crps.1), channel_id=1, replica_groups=mesh['chip'=32,'core'=2,'ens'=4] {'ens','chip'}, dimensions={0} | all-to-all | bytes 655360 | tf_op jit(solution)/shard_map/all_to_all | solution.py:264
  60.3 3.2 %collective-permute-start.1 = (bf16[128,2,640]{2,1,0:T(2,128)(2,1)S(1)}, bf16[128,2,640]{2,1,0:T(2,128)(2,1)S(1)}, u32[]{:S(2)}, u32[]{:S(2)}) collective-permute-start(bf16[128,2,640]{2,1,0:T(2,128)(2,1)S(1)} %all_to_all.10.own_ref), channel_id=1, source_target_pairs={{0,4},{4,0},{1,5},{5,1},{2,6},{6,2},{3,7},{7,3},{8,12},{12,8},{9,1... | collective-permute-start | bytes 983048 | tf_op jit(solution)/shard_map/ppermute | solution.py:268
  63.5 1.3 %collective-permute-done.1.partner_ref = bf16[128,2,640]{2,1,0:T(2,128)(2,1)S(1)} collective-permute-done((bf16[128,2,640]{2,1,0:T(2,128)(2,1)S(1)}, bf16[128,2,640]{2,1,0:T(2,128)(2,1)S(1)}, u32[]{:S(2)}, u32[]{:S(2)}) %collective-permute-start.1) | collective-permute-done | bytes 327712 | tf_op jit(solution)/shard_map/ppermute | solution.py:268
  64.8 0.0 copy-done
  64.8 2.4 %grid.1 = (bf16[576,1440]{1,0:T(8,128)(2,1)}, f32[2,2,36]{2,1,0:T(2,128)}) custom-call(s32[1]{0:T(128)} %bitcast.at_ref, bf16[128,2,640]{2,1,0:T(2,128)(2,1)S(1)} %all_to_all.10.own_ref, bf16[128,2,640]{2,1,0:T(2,128)(2,1)S(1)} %collective-permute-done.1.partner_ref, bf16[256,1440]{1,0:T(8,128)(2,1)S(1)} %copy-done), custom_call_target="tpu_custom_call" | custom-call | tf_op jit(solution)/shard_map/grid/pallas_call | solution.py:348
Async XLA Ops:
  0.6 35.3 %copy-start.1 = (s32[128]{0:T(128)S(1)}, s32[128]{0:T(128)}, u32[]{:S(2)}) copy-start(s32[128]{0:T(128)} %param.7) | copy-start | bytes 1540
  3.8 28.6 %all-to-all-start = ((bf16[128,2,640]{2,1,0:T(2,128)(2,1)}), bf16[128,2,640]{2,1,0:T(2,128)(2,1)S(1)}, u32[]{:S(2)}, u32[]{:S(2)}) async-start(bf16[128,2,640]{2,1,0:T(2,128)(2,1)} %get-tuple-element.11), calls=%async_computation | async-start | bytes 655360 | tf_op jit(solution)/shard_map/all_to_all | solution.py:264
  20.2 44.6 %copy-start = (bf16[256,1440]{1,0:T(8,128)(2,1)S(1)}, bf16[256,1440]{1,0:T(8,128)(2,1)}, u32[]{:S(2)}) copy-start(bf16[256,1440]{1,0:T(8,128)(2,1)} %get-tuple-element.17.table_ref) | copy-start | bytes 2211844
  32.4 4.8 %collective-permute-start = (bf16[128,2,640]{2,1,0:T(2,128)(2,1)S(1)}, bf16[128,2,640]{2,1,0:T(2,128)(2,1)S(1)}, u32[]{:S(2)}, u32[]{:S(2)}) collective-permute-start(bf16[128,2,640]{2,1,0:T(2,128)(2,1)S(1)} %all-to-all-done.own_ref), channel_id=1, source_target_pairs={{0,4},{4,0},{1,5},{5,1},{2,6},{6,2},{3,7},{7,3},{8,12},{12,8},{9,1... | collective-permute-start | bytes 983048 | tf_op jit(solution)/shard_map/ppermute | solution.py:268
  60.3 4.5 %collective-permute-start.1 = (bf16[128,2,640]{2,1,0:T(2,128)(2,1)S(1)}, bf16[128,2,640]{2,1,0:T(2,128)(2,1)S(1)}, u32[]{:S(2)}, u32[]{:S(2)}) collective-permute-start(bf16[128,2,640]{2,1,0:T(2,128)(2,1)S(1)} %all_to_all.10.own_ref), channel_id=1, source_target_pairs={{0,4},{4,0},{1,5},{5,1},{2,6},{6,2},{3,7},{7,3},{8,12},{12,8},{9,1... | collective-permute-start | bytes 983048 | tf_op jit(solution)/shard_map/ppermute | solution.py:268

commit v5 on v4

--- a/solution.py
+++ b/solution.py
@@ -114,9 +114,10 @@
     rows = lines // (2 * chips)
     source = lax.broadcasted_iota(jnp.int32, (lines, lines), 0)
     target = lax.broadcasted_iota(jnp.int32, (lines, lines), 1)
-    other = lax.rem(lax.div(target, chips), 2)
+    other = lax.div(target, lines // 2)
     their_core = core + other - 2 * core * other
-    line = rows * (2 * lax.rem(target, chips) + their_core) + lax.div(target, 2 * chips)
+    row = lax.div(lax.rem(target, lines // 2), chips)
+    line = rows * (2 * lax.rem(target, chips) + their_core) + row
     order = source == line
     turned = dot(mine[...], order.astype(F32).astype(BF16), ((1,), (0,)))
     basis_ref[...] = turned.astype(BF16)
@@ -142,24 +143,35 @@
     return parts
 
 
+def turn_lines(ref, q, turned, spectra, chips, ens, variables):
+    local = MEMBERS // ens
+    span = variables * 8
+    turned[...] = ref[:, q, :].astype(F32).T
+    for h in range(2):
+        for m in range(local):
+            parts = [turned[pl.ds(m * span + 4 * h + j, VROWS, stride=8), :] for j in range(4)]
+            for k, part in enumerate(swap_groups(parts, chips)):
+                e = k * local + m
+                spectra[pl.ds(e * VROWS, VROWS), pl.ds(h * LANES, LANES)] = part
+    return spectra[...].astype(BF16)
+
+
+def own_kernel(chips, ens, variables, own_ref, basis_ref, coeffs_ref, turned, spectra):
+    degrees, lines = basis_ref.shape
+    members = turn_lines(own_ref, 0, turned, spectra, chips, ens, variables)
+    coeffs_ref[:, :degrees] = dot(members, basis_ref[:, : lines // 2], ((1,), (1,)))
+
+
 def crps_kernel(
     chips, ens, degrees, variables,
-    z_ref, own_ref, partner_ref, obs_ref, basis_ref, send_ref,
+    z_ref, partner_ref, own_coeffs_ref, obs_ref, basis_ref, send_ref,
     turned, spectra, coeffs, grads, back,
 ):
     local = MEMBERS // ens
     span = variables * 8
-    for q, ref in enumerate((own_ref, partner_ref)):
-        turned[q] = ref[:, q, :].astype(F32).T
-    for t2 in range(4):
-        for m in range(local):
-            parts = [
-                turned[j % 2, pl.ds(m * span + 2 * t2 + j // 2, VROWS, stride=8), :] for j in range(4)
-            ]
-            for k, part in enumerate(swap_groups(parts, chips)):
-                e = k * local + m
-                spectra[pl.ds(e * VROWS, VROWS), pl.ds(t2 * LANES, LANES)] = part
-    coeffs[:, :degrees] = dot(spectra[...].astype(BF16), basis_ref[...], ((1,), (1,)))
+    half = basis_ref.shape[1] // 2
+    members = turn_lines(partner_ref, 1, turned, spectra, chips, ens, variables)
+    coeffs[:, :degrees] = own_coeffs_ref[:, :degrees] + dot(members, basis_ref[:, half:], ((1,), (1,)))
 
     zonal = z_ref[0]
     factor = jnp.where(zonal == 0, 1.0, 2.0).astype(F32)
@@ -209,13 +221,15 @@
 
     returned = dot(grads[:, :degrees], basis_ref[...], ((1,), (0,)))
     for m in range(local):
-        for t2 in range(4):
-            parts = []
-            for k in range(ens):
-                e = k * local + m
-                parts.append(returned[e * VROWS : (e + 1) * VROWS, t2 * LANES : (t2 + 1) * LANES])
-            for j, part in enumerate(swap_groups(parts, chips)):
-                back[j % 2, pl.ds(m * span + 2 * t2 + j // 2, VROWS, stride=8), :] = part
+        for q in range(2):
+            for h in range(2):
+                at = (2 * q + h) * LANES
+                parts = []
+                for k in range(ens):
+                    e = k * local + m
+                    parts.append(returned[e * VROWS : (e + 1) * VROWS, at : at + LANES])
+                for j, part in enumerate(swap_groups(parts, chips)):
+                    back[q, pl.ds(m * span + 4 * h + j, VROWS, stride=8), :] = part
     base = local * span
     for tile in range(tiles):
         rest = jnp.sum(totals[tile], axis=1, keepdims=True) * (1.0 / degrees)
@@ -228,20 +242,8 @@
         send_ref[:, q, :] = back[q].T.astype(BF16)
 
 
-def grid_kernel(chips, ens, variables, at_ref, own_ref, partner_ref, table_ref, out_ref, score_ref, block, sems):
-    rows, nodes = out_ref.shape
-    scale = nodes**-0.5
-    turned = jnp.concatenate(
-        [ref[:, q, :].astype(F32).T.astype(BF16) for q, ref in enumerate((own_ref, partner_ref))], axis=1
-    )
-    copies = []
-    for a in range(0, rows, LANES):
-        n = min(LANES, rows - a)
-        part = dot(turned[a : a + n, :], table_ref[...], ((1,), (0,))) * scale
-        block[a : a + n, :] = part.astype(BF16)
-        copy = pltpu.make_async_copy(block.at[pl.ds(a, n)], out_ref.at[pl.ds(a, n)], sems.at[len(copies)])
-        copy.start()
-        copies.append(copy)
+def score_kernel(chips, ens, variables, rows, at_ref, own_ref, turned_ref, score_ref):
+    turned_ref[...] = own_ref[:, 0, :].astype(F32).T.astype(BF16)
     base = WIDTH - LANES
     mine = lax.broadcasted_iota(jnp.int32, (chips, LANES), 0) == at_ref[0]
     for k in range(ens):
@@ -252,6 +254,21 @@
             total = term if total is None else total + term
         total = pltpu.roll(total, LANES - (rows - base), 1)
         score_ref[k % 2, k // 2 : k // 2 + 1, :] = total[:, :variables]
+
+
+def grid_kernel(partner_ref, own_ref, table_ref, out_ref, block, sems):
+    rows, nodes = out_ref.shape
+    scale = nodes**-0.5
+    partner = partner_ref[:, 1, :].astype(F32).T.astype(BF16)
+    turned = jnp.concatenate([own_ref[...], partner], axis=1)
+    copies = []
+    for a in range(0, rows, LANES):
+        n = min(LANES, rows - a)
+        part = dot(turned[a : a + n, :], table_ref[...], ((1,), (0,))) * scale
+        block[a : a + n, :] = part.astype(BF16)
+        copy = pltpu.make_async_copy(block.at[pl.ds(a, n)], out_ref.at[pl.ds(a, n)], sems.at[len(copies)])
+        copy.start()
+        copies.append(copy)
     for copy in copies:
         copy.wait()
 
@@ -327,6 +344,18 @@
     partner = from_partner(own)
     own_wave = lax.dynamic_slice_in_dim(zonal_order_values, 2 * (2 * chip + core) + slot, 1)
 
+    own_coeffs = pl.pallas_call(
+        functools.partial(own_kernel, chips, ens, variables),
+        name="own",
+        compiler_params=PARAMS,
+        in_specs=[whole, whole],
+        out_specs=whole,
+        out_shape=jax.ShapeDtypeStruct((MEMBERS * VROWS, padded), F32),
+        scratch_shapes=[VMEM((WIDTH, LANES), F32), VMEM((MEMBERS * VROWS, all_lines // 2), F32)],
+        cost_estimate=pl.CostEstimate(
+            flops=MEMBERS * VROWS * all_lines * degrees, bytes_accessed=2_000_000, transcendentals=0
+        ),
+    )(own, basis)
     send = pl.pallas_call(
         functools.partial(crps_kernel, chips, ens, degrees, variables),
         name="crps",
@@ -335,28 +364,37 @@
         out_specs=whole,
         out_shape=sent,
         scratch_shapes=[
-            VMEM((2, WIDTH, LANES), F32),
-            VMEM((MEMBERS * VROWS, all_lines), F32),
+            VMEM((WIDTH, LANES), F32),
+            VMEM((MEMBERS * VROWS, all_lines // 2), F32),
             VMEM((MEMBERS * VROWS, padded), F32),
             VMEM((MEMBERS * VROWS, padded), BF16),
             VMEM((2, WIDTH, LANES), F32),
         ],
-    )(own_wave, own, partner, observed, basis)
+    )(own_wave, partner, own_coeffs, observed, basis)
     own = to_chips(send)
     partner = from_partner(own)
 
-    sensitivity, scores = pl.pallas_call(
-        functools.partial(grid_kernel, chips, ens, variables),
-        name="grid",
-        compiler_params=PARAMS,
-        in_specs=[scalar, whole, whole, whole],
-        out_specs=[far, whole],
+    turned, scores = pl.pallas_call(
+        functools.partial(score_kernel, chips, ens, variables, rows),
+        name="score",
+        compiler_params=PARAMS,
+        in_specs=[scalar, whole],
+        out_specs=[whole, whole],
         out_shape=[
-            jax.ShapeDtypeStruct((rows, nodes), BF16),
+            jax.ShapeDtypeStruct((WIDTH, group), BF16),
             jax.ShapeDtypeStruct((2, 2, variables), F32),
         ],
+        cost_estimate=pl.CostEstimate(flops=20_000_000, bytes_accessed=500_000, transcendentals=0),
+    )(chip.reshape(1), own)
+    sensitivity = pl.pallas_call(
+        grid_kernel,
+        name="grid",
+        compiler_params=PARAMS,
+        in_specs=[whole, whole, whole],
+        out_specs=far,
+        out_shape=jax.ShapeDtypeStruct((rows, nodes), BF16),
         scratch_shapes=[VMEM((rows, nodes), BF16), pltpu.SemaphoreType.DMA((5,))],
-    )(chip.reshape(1), own, partner, table)
+    )(partner, turned, table)
     return sensitivity.reshape(predicted_grid.shape), scores.transpose(2, 0, 1)
 
 

time: 67.5 us -> 66.5 us (0.985)
  waiting for transfers between devices: 9.13 us -> 7.48 us
  Pallas kernels: 14.6 us -> 15.3 us
    ppermute x2, waiting for transfers between devices: 1.93 us -> 0.3 us  [from_partner(): return lax.ppermute(values, 'core', [(0, 1), (1, 0)])]
    pallas_call x1 -> x3, Pallas kernels: 2.43 us -> 3.28 us  [the longest x1 1.65 us: body(): pl.pallas_call(grid_kernel, name='grid', compiler_params=PARAMS, in_specs...]
  transfers between devices with their start and end apart: 3 -> 3, of which waited for: 3 -> 2; matrix products, arithmetic and copies ran while one was open for 1% -> 1% of each run, Pallas kernels for 7% -> 10%
where the time goes in v5:
time: 66.5 us; the launch traced here: 66.2 us
  starting transfers between devices  22.9 us (34%)
  blocking collectives  19.2 us (29%)
  Pallas kernels  15.3 us (23%)
  waiting for transfers between devices  7.48 us (11%)
  between operations  0.72 us (1%)
    all_to_all x1, blocking collectives, to_chips(): return lax.all_to_all(values, GROUP, 0, 0, tiled=True)  19.2 us
    all_to_all x1, starting transfers between devices, to_chips(): return lax.all_to_all(values, GROUP, 0, 0, tiled=True)  16.3 us
    all_to_all x1, waiting for transfers between devices, to_chips(): return lax.all_to_all(values, GROUP, 0, 0, tiled=True)  7.18 us
    ppermute x2, starting transfers between devices, from_partner(): return lax.ppermute(values, 'core', [(0, 1), (1, 0)])  6.53 us
    pallas_call x1, Pallas kernels, body(): pl.pallas_call(functools.partial(basis_kernel, chips), name='basis', comp...  4.95 us
    pallas_call x1, Pallas kernels, body(): pl.pallas_call(functools.partial(crps_kernel, chips, ens, degrees, variab...  3.93 us
    pallas_call x1, Pallas kernels, body(): pl.pallas_call(functools.partial(fourier_kernel, chips), name='fourier',...  3.13 us
    pallas_call x1, Pallas kernels, body(): pl.pallas_call(grid_kernel, name='grid', compiler_params=PARAMS, in_specs...  1.65 us
  transfers between devices with their start and end apart: 3, of which 2 were waited for; matrix products, arithmetic and copies ran while one was open for 1% of the time, Pallas kernels for 10%

profile of v5, /device:TPU:1, one launch (start us, length us, event | category | flops | bytes accessed | tf_op | source)
XLA Modules:
  0.0 66.2 jit_solution(3129699846326178366)
XLA Ops:
  0.6 0.0 copy-start.1
  0.6 3.1 %fourier.1 = (bf16[128,2,640]{2,1,0:T(2,128)(2,1)}, bf16[256,1440]{1,0:T(8,128)(2,1)}) custom-call(s32[1]{0:T(128)} %bitcast.core_ref, s32[1,128]{1,0:T(1,128)} %bitcast.12, bf16[576,1440]{1,0:T(8,128)(2,1)} %bitcast.9), custom_call_target="tpu_custom_call" | custom-call | tf_op jit(solution)/shard_map/fourier/pallas_call | solution.py:306
  3.8 16.3 %all-to-all-start = ((bf16[128,2,640]{2,1,0:T(2,128)(2,1)}), bf16[128,2,640]{2,1,0:T(2,128)(2,1)S(1)}, u32[]{:S(2)}, u32[]{:S(2)}) async-start(bf16[128,2,640]{2,1,0:T(2,128)(2,1)} %get-tuple-element.11), calls=%async_computation | async-start | bytes 655360 | tf_op jit(solution)/shard_map/all_to_all | solution.py:281
  20.2 0.1 pad_add_fusion.where_ref
  20.2 4.9 %basis.1 = (bf16[721,512]{1,0:T(8,128)(2,1)S(1)}, f32[40,768]{1,0:T(8,128)S(1)}) custom-call(s32[3]{0:T(128)S(1)} %pad_add_fusion.where_ref, bf16[721,2,512]{2,1,0:T(2,128)(2,1)} %bitcast.11, f32[36,2,2,721]{3,2,1,0:T(2,128)} %v_ref.1), custom_call_target="tpu_custom_call" | custom-call | flops 378011648 | bytes 4000000 | tf_op jit(solution)/shard_map/basis/pallas_call | solution.py:322
  25.2 7.2 %all-to-all-done.own_ref = bf16[128,2,640]{2,1,0:T(2,128)(2,1)S(1)} async-done(((bf16[128,2,640]{2,1,0:T(2,128)(2,1)}), bf16[128,2,640]{2,1,0:T(2,128)(2,1)S(1)}, u32[]{:S(2)}, u32[]{:S(2)}) %all-to-all-start) | async-done | bytes 327712 | tf_op jit(solution)/shard_map/all_to_all | solution.py:281
  32.4 3.6 %collective-permute-start = (bf16[128,2,640]{2,1,0:T(2,128)(2,1)S(1)}, bf16[128,2,640]{2,1,0:T(2,128)(2,1)S(1)}, u32[]{:S(2)}, u32[]{:S(2)}) collective-permute-start(bf16[128,2,640]{2,1,0:T(2,128)(2,1)S(1)} %all-to-all-done.own_ref), channel_id=1, source_target_pairs={{0,4},{4,0},{1,5},{5,1},{2,6},{6,2},{3,7},{7,3},{8,12},{12,8},{9,1... | collective-permute-start | bytes 983048 | tf_op jit(solution)/shard_map/ppermute | solution.py:285
  35.9 0.0 copy-done.1
  35.9 0.6 dynamic_slice.3.z_ref
  36.5 0.7 %own.1.own_coeffs_ref = f32[320,768]{1,0:T(8,128)S(1)} custom-call(bf16[128,2,640]{2,1,0:T(2,128)(2,1)S(1)} %all-to-all-done.own_ref, bf16[721,512]{1,0:T(8,128)(2,1)S(1)} %get-tuple-element.15.basis_ref), custom_call_target="tpu_custom_call" | custom-call | flops 118128640 | bytes 2000000 | tf_op jit(solution)/shard_map/own/pallas_call | solution.py:347
  37.2 0.0 copy-start
  37.2 0.0 collective-permute-done.partner_ref
  37.2 3.9 %crps.1 = bf16[128,2,640]{2,1,0:T(2,128)(2,1)S(1)} custom-call(s32[1]{0:T(128)} %dynamic_slice.3.z_ref, bf16[128,2,640]{2,1,0:T(2,128)(2,1)S(1)} %collective-permute-done.partner_ref, f32[320,768]{1,0:T(8,128)S(1)} %own.1.own_coeffs_ref, f32[40,768]{1,0:T(8,128)S(1)} %get-tuple-element.16.obs_ref, bf16[721,512]{1,0:T(8,128)(2,1)S(1)} %get-tuple-element.15.basis_ref), custom_call_target="tpu_custom_call" | custom-call | tf_op jit(solution)/shard_map/crps/pallas_call | solution.py:359
  41.2 19.2 %all_to_all.10.own_ref = bf16[128,2,640]{2,1,0:T(2,128)(2,1)S(1)} all-to-all(bf16[128,2,640]{2,1,0:T(2,128)(2,1)S(1)} %crps.1), channel_id=1, replica_groups=mesh['chip'=32,'core'=2,'ens'=4] {'ens','chip'}, dimensions={0} | all-to-all | bytes 655360 | tf_op jit(solution)/shard_map/all_to_all | solution.py:281
  60.3 3.0 %collective-permute-start.1 = (bf16[128,2,640]{2,1,0:T(2,128)(2,1)S(1)}, bf16[128,2,640]{2,1,0:T(2,128)(2,1)S(1)}, u32[]{:S(2)}, u32[]{:S(2)}) collective-permute-start(bf16[128,2,640]{2,1,0:T(2,128)(2,1)S(1)} %all_to_all.10.own_ref), channel_id=1, source_target_pairs={{0,4},{4,0},{1,5},{5,1},{2,6},{6,2},{3,7},{7,3},{8,12},{12,8},{9,1... | collective-permute-start | bytes 983048 | tf_op jit(solution)/shard_map/ppermute | solution.py:285
  63.3 1.0 %score.1 = (bf16[640,128]{1,0:T(8,128)(2,1)S(1)}, f32[2,2,36]{2,1,0:T(2,128)}) custom-call(s32[1]{0:T(128)} %bitcast.6.at_ref, bf16[128,2,640]{2,1,0:T(2,128)(2,1)S(1)} %all_to_all.10.own_ref), custom_call_target="tpu_custom_call" | custom-call | flops 20000000 | bytes 500000 | tf_op jit(solution)/shard_map/score/pallas_call | solution.py:377
  64.3 0.3 collective-permute-done.1.partner_ref
  64.6 0.0 copy-done
  64.6 1.7 %grid.1 = bf16[576,1440]{1,0:T(8,128)(2,1)} custom-call(bf16[128,2,640]{2,1,0:T(2,128)(2,1)S(1)} %collective-permute-done.1.partner_ref, bf16[640,128]{1,0:T(8,128)(2,1)S(1)} %get-tuple-element.17.own_ref, bf16[256,1440]{1,0:T(8,128)(2,1)S(1)} %copy-done), custom_call_target="tpu_custom_call" | custom-call | tf_op jit(solution)/shard_map/grid/pallas_call | solution.py:389
Async XLA Ops:
  0.6 35.3 %copy-start.1 = (s32[128]{0:T(128)S(1)}, s32[128]{0:T(128)}, u32[]{:S(2)}) copy-start(s32[128]{0:T(128)} %param.7) | copy-start | bytes 1540
  3.8 28.6 %all-to-all-start = ((bf16[128,2,640]{2,1,0:T(2,128)(2,1)}), bf16[128,2,640]{2,1,0:T(2,128)(2,1)S(1)}, u32[]{:S(2)}, u32[]{:S(2)}) async-start(bf16[128,2,640]{2,1,0:T(2,128)(2,1)} %get-tuple-element.11), calls=%async_computation | async-start | bytes 655360 | tf_op jit(solution)/shard_map/all_to_all | solution.py:281
  32.4 4.8 %collective-permute-start = (bf16[128,2,640]{2,1,0:T(2,128)(2,1)S(1)}, bf16[128,2,640]{2,1,0:T(2,128)(2,1)S(1)}, u32[]{:S(2)}, u32[]{:S(2)}) collective-permute-start(bf16[128,2,640]{2,1,0:T(2,128)(2,1)S(1)} %all-to-all-done.own_ref), channel_id=1, source_target_pairs={{0,4},{4,0},{1,5},{5,1},{2,6},{6,2},{3,7},{7,3},{8,12},{12,8},{9,1... | collective-permute-start | bytes 983048 | tf_op jit(solution)/shard_map/ppermute | solution.py:285
  37.2 27.4 %copy-start = (bf16[256,1440]{1,0:T(8,128)(2,1)S(1)}, bf16[256,1440]{1,0:T(8,128)(2,1)}, u32[]{:S(2)}) copy-start(bf16[256,1440]{1,0:T(8,128)(2,1)} %get-tuple-element.18.table_ref) | copy-start | bytes 2211844
  60.3 4.2 %collective-permute-start.1 = (bf16[128,2,640]{2,1,0:T(2,128)(2,1)S(1)}, bf16[128,2,640]{2,1,0:T(2,128)(2,1)S(1)}, u32[]{:S(2)}, u32[]{:S(2)}) collective-permute-start(bf16[128,2,640]{2,1,0:T(2,128)(2,1)S(1)} %all_to_all.10.own_ref), channel_id=1, source_target_pairs={{0,4},{4,0},{1,5},{5,1},{2,6},{6,2},{3,7},{7,3},{8,12},{12,8},{9,1... | collective-permute-start | bytes 983048 | tf_op jit(solution)/shard_map/ppermute | solution.py:285

commit v6 on v5

--- a/solution.py
+++ b/solution.py
@@ -120,7 +120,8 @@
     line = rows * (2 * lax.rem(target, chips) + their_core) + row
     order = source == line
     turned = dot(mine[...], order.astype(F32).astype(BF16), ((1,), (0,)))
-    basis_ref[...] = turned.astype(BF16)
+    basis_ref[:degrees, :] = turned.astype(BF16)
+    basis_ref[degrees:, :] = jnp.zeros((basis_ref.shape[0] - degrees, lines), BF16)
     second.wait()
     seen = v_vmem[...]
     obs_ref[...] = jnp.zeros(obs_ref.shape, F32)
@@ -157,9 +158,9 @@
 
 
 def own_kernel(chips, ens, variables, own_ref, basis_ref, coeffs_ref, turned, spectra):
-    degrees, lines = basis_ref.shape
+    lines = basis_ref.shape[1]
     members = turn_lines(own_ref, 0, turned, spectra, chips, ens, variables)
-    coeffs_ref[:, :degrees] = dot(members, basis_ref[:, : lines // 2], ((1,), (1,)))
+    coeffs_ref[...] = dot(members, basis_ref[:, : lines // 2], ((1,), (1,)))
 
 
 def crps_kernel(
@@ -171,7 +172,7 @@
     span = variables * 8
     half = basis_ref.shape[1] // 2
     members = turn_lines(partner_ref, 1, turned, spectra, chips, ens, variables)
-    coeffs[:, :degrees] = own_coeffs_ref[:, :degrees] + dot(members, basis_ref[:, half:], ((1,), (1,)))
+    coeffs[...] = own_coeffs_ref[...] + dot(members, basis_ref[:, half:], ((1,), (1,)))
 
     zonal = z_ref[0]
     factor = jnp.where(zonal == 0, 1.0, 2.0).astype(F32)
@@ -187,19 +188,20 @@
             seen = obs_ref[pl.ds(tile * 8, 8), lanes]
             slope = [None] * MEMBERS
             spread = None
+            inverses = None
             for e in range(MEMBERS - 1):
-                part = None
                 for f in range(e + 1, MEMBERS):
                     gap = c[e] - c[f]
-                    square = gap * gap + SMOOTH * SMOOTH
-                    inverse = lax.rsqrt(square)
+                    inverse = lax.rsqrt(gap * gap + SMOOTH * SMOOTH)
                     sign = gap * inverse
-                    root = square * inverse
-                    part = root if part is None else part + root
+                    inverses = inverse if inverses is None else inverses + inverse
                     slope[e] = sign if slope[e] is None else slope[e] + sign
                     slope[f] = -sign if slope[f] is None else slope[f] - sign
-                part = part - SMOOTH * (MEMBERS - 1 - e)
+            for e in range(1, MEMBERS):
+                part = (c[e] - c[0]) * slope[e]
                 spread = part if spread is None else spread + part
+            pairs = MEMBERS * (MEMBERS - 1) // 2
+            spread = spread + (inverses * (SMOOTH * SMOOTH) - SMOOTH * pairs)
             miss = None
             for e in range(MEMBERS):
                 gap = c[e] - seen
@@ -217,9 +219,9 @@
 
     blocks = coeffs.shape[1] // LANES
     zero = jnp.zeros((8, LANES), F32)
-    totals = lax.fori_loop(0, blocks, one_block, (zero,) * tiles)
-
-    returned = dot(grads[:, :degrees], basis_ref[...], ((1,), (0,)))
+    totals = lax.fori_loop(0, blocks, one_block, (zero,) * tiles, unroll=6)
+
+    returned = dot(grads[...], basis_ref[...], ((1,), (0,)))
     for m in range(local):
         for q in range(2):
             for h in range(2):
@@ -326,7 +328,7 @@
         in_specs=[scalar, far, far],
         out_specs=[whole, whole],
         out_shape=[
-            jax.ShapeDtypeStruct((degrees, all_lines), BF16),
+            jax.ShapeDtypeStruct((padded, all_lines), BF16),
             jax.ShapeDtypeStruct((VROWS, padded), F32),
         ],
         scratch_shapes=[

time: 66.5 us -> 66.2 us (level)
  no operation moved by 1% of the time
where the time goes in v6:
time: 66.2 us; the launch traced here: 66 us
  starting transfers between devices  22.9 us (35%)
  blocking collectives  19.2 us (29%)
  Pallas kernels  15.1 us (23%)
  waiting for transfers between devices  7.48 us (11%)
  between operations  0.71 us (1%)
    all_to_all x1, blocking collectives, to_chips(): return lax.all_to_all(values, GROUP, 0, 0, tiled=True)  19.2 us
    all_to_all x1, starting transfers between devices, to_chips(): return lax.all_to_all(values, GROUP, 0, 0, tiled=True)  16.3 us
    all_to_all x1, waiting for transfers between devices, to_chips(): return lax.all_to_all(values, GROUP, 0, 0, tiled=True)  7.18 us
    ppermute x2, starting transfers between devices, from_partner(): return lax.ppermute(values, 'core', [(0, 1), (1, 0)])  6.53 us
    pallas_call x1, Pallas kernels, body(): pl.pallas_call(functools.partial(basis_kernel, chips), name='basis', comp...  4.95 us
    pallas_call x1, Pallas kernels, body(): pl.pallas_call(functools.partial(crps_kernel, chips, ens, degrees, variab...  3.71 us
    pallas_call x1, Pallas kernels, body(): pl.pallas_call(functools.partial(fourier_kernel, chips), name='fourier',...  3.13 us
    pallas_call x1, Pallas kernels, body(): pl.pallas_call(grid_kernel, name='grid', compiler_params=PARAMS, in_specs...  1.65 us
  transfers between devices with their start and end apart: 3, of which 2 were waited for; matrix products, arithmetic and copies ran while one was open for 1% of the time, Pallas kernels for 10%

profile of v6, /device:TPU:1, one launch (start us, length us, event | category | flops | bytes accessed | tf_op | source)
XLA Modules:
  0.0 66.0 jit_solution(10782123631347358733)
XLA Ops:
  0.6 0.0 copy-start.1
  0.6 3.1 %fourier.1 = (bf16[128,2,640]{2,1,0:T(2,128)(2,1)}, bf16[256,1440]{1,0:T(8,128)(2,1)}) custom-call(s32[1]{0:T(128)} %bitcast.core_ref, s32[1,128]{1,0:T(1,128)} %bitcast.12, bf16[576,1440]{1,0:T(8,128)(2,1)} %bitcast.9), custom_call_target="tpu_custom_call" | custom-call | tf_op jit(solution)/shard_map/fourier/pallas_call | solution.py:308
  3.8 16.3 %all-to-all-start = ((bf16[128,2,640]{2,1,0:T(2,128)(2,1)}), bf16[128,2,640]{2,1,0:T(2,128)(2,1)S(1)}, u32[]{:S(2)}, u32[]{:S(2)}) async-start(bf16[128,2,640]{2,1,0:T(2,128)(2,1)} %get-tuple-element.11), calls=%async_computation | async-start | bytes 655360 | tf_op jit(solution)/shard_map/all_to_all | solution.py:283
  20.2 0.1 pad_add_fusion.where_ref
  20.2 5.0 %basis.1 = (bf16[768,512]{1,0:T(8,128)(2,1)S(1)}, f32[40,768]{1,0:T(8,128)S(1)}) custom-call(s32[3]{0:T(128)S(1)} %pad_add_fusion.where_ref, bf16[721,2,512]{2,1,0:T(2,128)(2,1)} %bitcast.11, f32[36,2,2,721]{3,2,1,0:T(2,128)} %v_ref.1), custom_call_target="tpu_custom_call" | custom-call | flops 378011648 | bytes 4000000 | tf_op jit(solution)/shard_map/basis/pallas_call | solution.py:324
  25.2 7.2 %all-to-all-done.own_ref = bf16[128,2,640]{2,1,0:T(2,128)(2,1)S(1)} async-done(((bf16[128,2,640]{2,1,0:T(2,128)(2,1)}), bf16[128,2,640]{2,1,0:T(2,128)(2,1)S(1)}, u32[]{:S(2)}, u32[]{:S(2)}) %all-to-all-start) | async-done | bytes 327712 | tf_op jit(solution)/shard_map/all_to_all | solution.py:283
  32.4 3.6 %collective-permute-start = (bf16[128,2,640]{2,1,0:T(2,128)(2,1)S(1)}, bf16[128,2,640]{2,1,0:T(2,128)(2,1)S(1)}, u32[]{:S(2)}, u32[]{:S(2)}) collective-permute-start(bf16[128,2,640]{2,1,0:T(2,128)(2,1)S(1)} %all-to-all-done.own_ref), channel_id=1, source_target_pairs={{0,4},{4,0},{1,5},{5,1},{2,6},{6,2},{3,7},{7,3},{8,12},{12,8},{9,1... | collective-permute-start | bytes 983048 | tf_op jit(solution)/shard_map/ppermute | solution.py:287
  35.9 0.0 copy-done.1
  35.9 0.6 dynamic_slice.3.z_ref
  36.5 0.7 %own.1.own_coeffs_ref = f32[320,768]{1,0:T(8,128)S(1)} custom-call(bf16[128,2,640]{2,1,0:T(2,128)(2,1)S(1)} %all-to-all-done.own_ref, bf16[768,512]{1,0:T(8,128)(2,1)S(1)} %get-tuple-element.15.basis_ref), custom_call_target="tpu_custom_call" | custom-call | flops 118128640 | bytes 2000000 | tf_op jit(solution)/shard_map/own/pallas_call | solution.py:349
  37.2 0.0 copy-start
  37.2 0.0 collective-permute-done.partner_ref
  37.2 3.7 %crps.1 = bf16[128,2,640]{2,1,0:T(2,128)(2,1)S(1)} custom-call(s32[1]{0:T(128)} %dynamic_slice.3.z_ref, bf16[128,2,640]{2,1,0:T(2,128)(2,1)S(1)} %collective-permute-done.partner_ref, f32[320,768]{1,0:T(8,128)S(1)} %own.1.own_coeffs_ref, f32[40,768]{1,0:T(8,128)S(1)} %get-tuple-element.16.obs_ref, bf16[768,512]{1,0:T(8,128)(2,1)S(1)} %get-tuple-element.15.basis_ref), custom_call_target="tpu_custom_call" | custom-call | tf_op jit(solution)/shard_map/crps/pallas_call | solution.py:361
  40.9 19.2 %all_to_all.10.own_ref = bf16[128,2,640]{2,1,0:T(2,128)(2,1)S(1)} all-to-all(bf16[128,2,640]{2,1,0:T(2,128)(2,1)S(1)} %crps.1), channel_id=1, replica_groups=mesh['chip'=32,'core'=2,'ens'=4] {'ens','chip'}, dimensions={0} | all-to-all | bytes 655360 | tf_op jit(solution)/shard_map/all_to_all | solution.py:283
  60.1 3.0 %collective-permute-start.1 = (bf16[128,2,640]{2,1,0:T(2,128)(2,1)S(1)}, bf16[128,2,640]{2,1,0:T(2,128)(2,1)S(1)}, u32[]{:S(2)}, u32[]{:S(2)}) collective-permute-start(bf16[128,2,640]{2,1,0:T(2,128)(2,1)S(1)} %all_to_all.10.own_ref), channel_id=1, source_target_pairs={{0,4},{4,0},{1,5},{5,1},{2,6},{6,2},{3,7},{7,3},{8,12},{12,8},{9,1... | collective-permute-start | bytes 983048 | tf_op jit(solution)/shard_map/ppermute | solution.py:287
  63.1 1.0 %score.1 = (bf16[640,128]{1,0:T(8,128)(2,1)S(1)}, f32[2,2,36]{2,1,0:T(2,128)}) custom-call(s32[1]{0:T(128)} %bitcast.6.at_ref, bf16[128,2,640]{2,1,0:T(2,128)(2,1)S(1)} %all_to_all.10.own_ref), custom_call_target="tpu_custom_call" | custom-call | flops 20000000 | bytes 500000 | tf_op jit(solution)/shard_map/score/pallas_call | solution.py:379
  64.0 0.3 collective-permute-done.1.partner_ref
  64.3 0.0 copy-done
  64.3 1.7 %grid.1 = bf16[576,1440]{1,0:T(8,128)(2,1)} custom-call(bf16[128,2,640]{2,1,0:T(2,128)(2,1)S(1)} %collective-permute-done.1.partner_ref, bf16[640,128]{1,0:T(8,128)(2,1)S(1)} %get-tuple-element.17.own_ref, bf16[256,1440]{1,0:T(8,128)(2,1)S(1)} %copy-done), custom_call_target="tpu_custom_call" | custom-call | tf_op jit(solution)/shard_map/grid/pallas_call | solution.py:391
Async XLA Ops:
  0.6 35.3 %copy-start.1 = (s32[128]{0:T(128)S(1)}, s32[128]{0:T(128)}, u32[]{:S(2)}) copy-start(s32[128]{0:T(128)} %param.7) | copy-start | bytes 1540
  3.8 28.6 %all-to-all-start = ((bf16[128,2,640]{2,1,0:T(2,128)(2,1)}), bf16[128,2,640]{2,1,0:T(2,128)(2,1)S(1)}, u32[]{:S(2)}, u32[]{:S(2)}) async-start(bf16[128,2,640]{2,1,0:T(2,128)(2,1)} %get-tuple-element.11), calls=%async_computation | async-start | bytes 655360 | tf_op jit(solution)/shard_map/all_to_all | solution.py:283
  32.4 4.8 %collective-permute-start = (bf16[128,2,640]{2,1,0:T(2,128)(2,1)S(1)}, bf16[128,2,640]{2,1,0:T(2,128)(2,1)S(1)}, u32[]{:S(2)}, u32[]{:S(2)}) collective-permute-start(bf16[128,2,640]{2,1,0:T(2,128)(2,1)S(1)} %all-to-all-done.own_ref), channel_id=1, source_target_pairs={{0,4},{4,0},{1,5},{5,1},{2,6},{6,2},{3,7},{7,3},{8,12},{12,8},{9,1... | collective-permute-start | bytes 983048 | tf_op jit(solution)/shard_map/ppermute | solution.py:287
  37.2 27.1 %copy-start = (bf16[256,1440]{1,0:T(8,128)(2,1)S(1)}, bf16[256,1440]{1,0:T(8,128)(2,1)}, u32[]{:S(2)}) copy-start(bf16[256,1440]{1,0:T(8,128)(2,1)} %get-tuple-element.18.table_ref) | copy-start | bytes 2211844
  60.1 4.2 %collective-permute-start.1 = (bf16[128,2,640]{2,1,0:T(2,128)(2,1)S(1)}, bf16[128,2,640]{2,1,0:T(2,128)(2,1)S(1)}, u32[]{:S(2)}, u32[]{:S(2)}) collective-permute-start(bf16[128,2,640]{2,1,0:T(2,128)(2,1)S(1)} %all_to_all.10.own_ref), channel_id=1, source_target_pairs={{0,4},{4,0},{1,5},{5,1},{2,6},{6,2},{3,7},{7,3},{8,12},{12,8},{9,1... | collective-permute-start | bytes 983048 | tf_op jit(solution)/shard_map/ppermute | solution.py:287

commit v7 on v6

--- a/solution.py
+++ b/solution.py
@@ -342,9 +342,9 @@
         jnp.stack([slot, at_ens % 2, core]),
         *far_of(weighted_polynomial_values.transpose(2, 0, 1), verifying_coefficients),
     )
-    own, basis, observed = lax.optimization_barrier((own, basis, observed))
+    own_wave = lax.dynamic_slice_in_dim(zonal_order_values, 2 * (2 * chip + core) + slot, 1)
+    own, basis, observed, own_wave = lax.optimization_barrier((own, basis, observed, own_wave))
     partner = from_partner(own)
-    own_wave = lax.dynamic_slice_in_dim(zonal_order_values, 2 * (2 * chip + core) + slot, 1)
 
     own_coeffs = pl.pallas_call(
         functools.partial(own_kernel, chips, ens, variables),

time: 66.2 us -> 66.2 us (level)
  transfers between devices with their start and end apart: 3 -> 3, of which waited for: 2 -> 3; matrix products, arithmetic and copies ran while one was open for 1% -> 1% of each run, Pallas kernels for 10% -> 10%
where the time goes in v7:
time: 66.2 us; the launch traced here: 65.9 us
  starting transfers between devices  23.2 us (35%)
  blocking collectives  18.9 us (29%)
  Pallas kernels  15 us (23%)
  waiting for transfers between devices  7.4 us (11%)
  between operations  0.73 us (1%)
    all_to_all x1, blocking collectives, to_chips(): return lax.all_to_all(values, GROUP, 0, 0, tiled=True)  18.9 us
    all_to_all x1, starting transfers between devices, to_chips(): return lax.all_to_all(values, GROUP, 0, 0, tiled=True)  16.3 us
    ppermute x2, starting transfers between devices, from_partner(): return lax.ppermute(values, 'core', [(0, 1), (1, 0)])  6.83 us
    all_to_all x1, waiting for transfers between devices, to_chips(): return lax.all_to_all(values, GROUP, 0, 0, tiled=True)  6.54 us
    pallas_call x1, Pallas kernels, body(): pl.pallas_call(functools.partial(basis_kernel, chips), name='basis', comp...  4.95 us
    pallas_call x1, Pallas kernels, body(): pl.pallas_call(functools.partial(crps_kernel, chips, ens, degrees, variab...  3.62 us
    pallas_call x1, Pallas kernels, body(): pl.pallas_call(functools.partial(fourier_kernel, chips), name='fourier',...  3.13 us
    pallas_call x1, Pallas kernels, body(): pl.pallas_call(grid_kernel, name='grid', compiler_params=PARAMS, in_specs...  1.65 us
  transfers between devices with their start and end apart: 3, of which 3 were waited for; matrix products, arithmetic and copies ran while one was open for 1% of the time, Pallas kernels for 10%

profile of v7, /device:TPU:1, one launch (start us, length us, event | category | flops | bytes accessed | tf_op | source)
XLA Modules:
  0.0 65.9 jit_solution(14106672528950168629)
XLA Ops:
  0.6 0.0 copy-start.1
  0.6 3.1 %fourier.1 = (bf16[128,2,640]{2,1,0:T(2,128)(2,1)}, bf16[256,1440]{1,0:T(8,128)(2,1)}) custom-call(s32[1]{0:T(128)} %bitcast.core_ref, s32[1,128]{1,0:T(1,128)} %bitcast.12, bf16[576,1440]{1,0:T(8,128)(2,1)} %bitcast.9), custom_call_target="tpu_custom_call" | custom-call | tf_op jit(solution)/shard_map/fourier/pallas_call | solution.py:308
  3.8 16.3 %all-to-all-start = ((bf16[128,2,640]{2,1,0:T(2,128)(2,1)}), bf16[128,2,640]{2,1,0:T(2,128)(2,1)S(1)}, u32[]{:S(2)}, u32[]{:S(2)}) async-start(bf16[128,2,640]{2,1,0:T(2,128)(2,1)} %get-tuple-element.12), calls=%async_computation | async-start | bytes 655360 | tf_op jit(solution)/shard_map/all_to_all | solution.py:283
  20.2 0.0 copy-done.1
  20.2 0.6 dynamic_slice.3.z_ref
  20.8 0.1 pad_add_fusion.where_ref
  20.8 4.9 %basis.1 = (bf16[768,512]{1,0:T(8,128)(2,1)S(1)}, f32[40,768]{1,0:T(8,128)S(1)}) custom-call(s32[3]{0:T(128)S(1)} %pad_add_fusion.where_ref, bf16[721,2,512]{2,1,0:T(2,128)(2,1)} %bitcast.11, f32[36,2,2,721]{3,2,1,0:T(2,128)} %v_ref.1), custom_call_target="tpu_custom_call" | custom-call | flops 378011648 | bytes 4000000 | tf_op jit(solution)/shard_map/basis/pallas_call | solution.py:324
  25.8 6.5 %all-to-all-done.own_ref = bf16[128,2,640]{2,1,0:T(2,128)(2,1)S(1)} async-done(((bf16[128,2,640]{2,1,0:T(2,128)(2,1)}), bf16[128,2,640]{2,1,0:T(2,128)(2,1)S(1)}, u32[]{:S(2)}, u32[]{:S(2)}) %all-to-all-start) | async-done | bytes 327712 | tf_op jit(solution)/shard_map/all_to_all | solution.py:283
  32.3 3.6 %collective-permute-start = (bf16[128,2,640]{2,1,0:T(2,128)(2,1)S(1)}, bf16[128,2,640]{2,1,0:T(2,128)(2,1)S(1)}, u32[]{:S(2)}, u32[]{:S(2)}) collective-permute-start(bf16[128,2,640]{2,1,0:T(2,128)(2,1)S(1)} %all-to-all-done.own_ref), channel_id=1, source_target_pairs={{0,4},{4,0},{1,5},{5,1},{2,6},{6,2},{3,7},{7,3},{8,12},{12,8},{9,1... | collective-permute-start | bytes 983048 | tf_op jit(solution)/shard_map/ppermute | solution.py:287
  35.9 0.7 %own.1.own_coeffs_ref = f32[320,768]{1,0:T(8,128)S(1)} custom-call(bf16[128,2,640]{2,1,0:T(2,128)(2,1)S(1)} %all-to-all-done.own_ref, bf16[768,512]{1,0:T(8,128)(2,1)S(1)} %get-tuple-element.17.basis_ref), custom_call_target="tpu_custom_call" | custom-call | flops 118128640 | bytes 2000000 | tf_op jit(solution)/shard_map/own/pallas_call | solution.py:349
  36.6 0.0 copy-start
  36.6 0.6 collective-permute-done.partner_ref
  37.2 3.6 %crps.1 = bf16[128,2,640]{2,1,0:T(2,128)(2,1)S(1)} custom-call(s32[1]{0:T(128)} %dynamic_slice.3.z_ref, bf16[128,2,640]{2,1,0:T(2,128)(2,1)S(1)} %collective-permute-done.partner_ref, f32[320,768]{1,0:T(8,128)S(1)} %own.1.own_coeffs_ref, f32[40,768]{1,0:T(8,128)S(1)} %get-tuple-element.18.obs_ref, bf16[768,512]{1,0:T(8,128)(2,1)S(1)} %get-tuple-element.17.basis_ref), custom_call_target="tpu_custom_call" | custom-call | tf_op jit(solution)/shard_map/crps/pallas_call | solution.py:361
  40.8 18.9 %all_to_all.10.own_ref = bf16[128,2,640]{2,1,0:T(2,128)(2,1)S(1)} all-to-all(bf16[128,2,640]{2,1,0:T(2,128)(2,1)S(1)} %crps.1), channel_id=1, replica_groups=mesh['chip'=32,'core'=2,'ens'=4] {'ens','chip'}, dimensions={0} | all-to-all | bytes 655360 | tf_op jit(solution)/shard_map/all_to_all | solution.py:283
  59.8 3.2 %collective-permute-start.1 = (bf16[128,2,640]{2,1,0:T(2,128)(2,1)S(1)}, bf16[128,2,640]{2,1,0:T(2,128)(2,1)S(1)}, u32[]{:S(2)}, u32[]{:S(2)}) collective-permute-start(bf16[128,2,640]{2,1,0:T(2,128)(2,1)S(1)} %all_to_all.10.own_ref), channel_id=1, source_target_pairs={{0,4},{4,0},{1,5},{5,1},{2,6},{6,2},{3,7},{7,3},{8,12},{12,8},{9,1... | collective-permute-start | bytes 983048 | tf_op jit(solution)/shard_map/ppermute | solution.py:287
  63.0 1.0 %score.1 = (bf16[640,128]{1,0:T(8,128)(2,1)S(1)}, f32[2,2,36]{2,1,0:T(2,128)}) custom-call(s32[1]{0:T(128)} %bitcast.6.at_ref, bf16[128,2,640]{2,1,0:T(2,128)(2,1)S(1)} %all_to_all.10.own_ref), custom_call_target="tpu_custom_call" | custom-call | flops 20000000 | bytes 500000 | tf_op jit(solution)/shard_map/score/pallas_call | solution.py:379
  64.0 0.3 collective-permute-done.1.partner_ref
  64.3 0.0 copy-done
  64.3 1.7 %grid.1 = bf16[576,1440]{1,0:T(8,128)(2,1)} custom-call(bf16[128,2,640]{2,1,0:T(2,128)(2,1)S(1)} %collective-permute-done.1.partner_ref, bf16[640,128]{1,0:T(8,128)(2,1)S(1)} %get-tuple-element.19.own_ref, bf16[256,1440]{1,0:T(8,128)(2,1)S(1)} %copy-done), custom_call_target="tpu_custom_call" | custom-call | tf_op jit(solution)/shard_map/grid/pallas_call | solution.py:391
Async XLA Ops:
  0.6 19.5 %copy-start.1 = (s32[128]{0:T(128)S(1)}, s32[128]{0:T(128)}, u32[]{:S(2)}) copy-start(s32[128]{0:T(128)} %param.7) | copy-start | bytes 1540
  3.8 28.6 %all-to-all-start = ((bf16[128,2,640]{2,1,0:T(2,128)(2,1)}), bf16[128,2,640]{2,1,0:T(2,128)(2,1)S(1)}, u32[]{:S(2)}, u32[]{:S(2)}) async-start(bf16[128,2,640]{2,1,0:T(2,128)(2,1)} %get-tuple-element.12), calls=%async_computation | async-start | bytes 655360 | tf_op jit(solution)/shard_map/all_to_all | solution.py:283
  32.3 4.8 %collective-permute-start = (bf16[128,2,640]{2,1,0:T(2,128)(2,1)S(1)}, bf16[128,2,640]{2,1,0:T(2,128)(2,1)S(1)}, u32[]{:S(2)}, u32[]{:S(2)}) collective-permute-start(bf16[128,2,640]{2,1,0:T(2,128)(2,1)S(1)} %all-to-all-done.own_ref), channel_id=1, source_target_pairs={{0,4},{4,0},{1,5},{5,1},{2,6},{6,2},{3,7},{7,3},{8,12},{12,8},{9,1... | collective-permute-start | bytes 983048 | tf_op jit(solution)/shard_map/ppermute | solution.py:287
  36.6 27.6 %copy-start = (bf16[256,1440]{1,0:T(8,128)(2,1)S(1)}, bf16[256,1440]{1,0:T(8,128)(2,1)}, u32[]{:S(2)}) copy-start(bf16[256,1440]{1,0:T(8,128)(2,1)} %get-tuple-element.20.table_ref) | copy-start | bytes 2211844
  59.8 4.5 %collective-permute-start.1 = (bf16[128,2,640]{2,1,0:T(2,128)(2,1)S(1)}, bf16[128,2,640]{2,1,0:T(2,128)(2,1)S(1)}, u32[]{:S(2)}, u32[]{:S(2)}) collective-permute-start(bf16[128,2,640]{2,1,0:T(2,128)(2,1)S(1)} %all_to_all.10.own_ref), channel_id=1, source_target_pairs={{0,4},{4,0},{1,5},{5,1},{2,6},{6,2},{3,7},{7,3},{8,12},{12,8},{9,1... | collective-permute-start | bytes 983048 | tf_op jit(solution)/shard_map/ppermute | solution.py:287
